TPU v7x, 128 devices: a whole 4x4x4 slice. The times are simulated.
128 devices in a mesh: row: 8 (over z, y_hi), col: 16 (over y_lo, x, core).
Axes of the slice: x: 4, y: 4 (y_hi: 2, y_lo: 2; y = y_hi * 2 + y_lo), z: 4, core: 2. Of those that a mesh axis runs over, the one named last changes fastest.
Arguments:
- matrix_tiles: float32 [8, 16, 16, 512, 512], P('row', 'col'), may hold values from -0.25 to 0.25
- tile_rows: int32 [8, 16, 16], P('row', 'col'), may hold values from 0 to 127, as said below
- tile_columns: int32 [8, 16, 16], P('row', 'col'), may hold values from 0 to 63, as said below
- tile_counts: int32 [8, 16], P('row', 'col'), may hold values from 8 to 16, as said below
- primal_iter: float32 [2, 524288], P(None, ('col', 'row')), may hold values from -6 to 6
- dual_iter: float32 [2, 524288], P(None, ('row', 'col')), may hold values from -6 to 6
- requirement: float32 [524288], P('row'), may hold values from -68 to 68
- constraint_kind: int32 [524288], P('row'), may hold values from 0 to 1
- objective: float32 [524288], P('col'), may hold values from -68 to 68
- lower_bound: float32 [524288], P('col'), may hold values from -1.5 to 1.5
- upper_bound: float32 [524288], P('col'), may hold values from -1.5 to 1.5
- variable_kind: int32 [524288], P('col'), may hold values from 0 to 3
Outputs:
- primal_residual: float32 [2, 524288], P(None, ('row', 'col'))
- dual_residual: float32 [2, 524288], P(None, ('col', 'row'))
- metrics: float32 [2, 3], replicated
Inputs may be any that keep to these rules, and one draw needn't show every extreme that they name: `tile_counts`: slots below the count of a list hold live tiles, the others are padding; some list has all 16 slots live. `tile_rows`: in each constraint group, the first (8) slots of its lists name every block row of the group exactly once; later slots name any block row, and repeated tiles add. `tile_columns`: in each variable group, the first (8) slots of its lists name every block column of the group exactly once; later slots name any block column, and repeated tiles add. `constraint_kind`: 0 marks an equality, 1 a constraint of the form at least. `variable_kind`: 0 free, 1 lower bound only, 2 upper bound only, 3 both bounds.
All inputs are finite; a program needn't handle non-finite values.
Results may differ from a plain program's by a relative error of at most 0.0003.
Values sent between devices are 32-bit elements; how exact they have to be, the bound alone decides.
A program may use at most 64 MiB of HBM per device.

v0:
```python
import jax
import jax.numpy as jnp
from jax import lax
from jax.sharding import Mesh
from jax.sharding import PartitionSpec as P

ROW = ("row_0", "row_1")
COL = ("col_0", "col_1", "col_2")
ROW_COL = ("row_0", "row_1", "col_0", "col_1", "col_2")
COL_ROW = ("col_0", "col_1", "col_2", "row_0", "row_1")


HIGHEST_PRECISION = lax.Precision.HIGHEST


def from_everyone(shard, axis):
    copies = jnp.broadcast_to(shard, (lax.axis_size(axis), *shard.shape))
    return lax.all_to_all(copies, axis, split_axis=0, concat_axis=0, tiled=True)


def joined_along(pieces, dim):
    lengths = list(pieces.shape[1:])
    lengths[dim] *= pieces.shape[0]
    return jnp.moveaxis(pieces, 0, dim).reshape(lengths)


def collect(shard, axis, dim):
    pieces = from_everyone(shard, axis)
    return joined_along(pieces, dim)


def cut_along(shard, dim, count):
    lengths = shard.shape
    pieces = shard.reshape(*lengths[:dim], count, lengths[dim] // count, *lengths[dim + 1 :])
    return jnp.moveaxis(pieces, dim, 0)


def sum_at_owner(shard, axis, dim):
    count = lax.axis_size(axis)
    pieces = lax.all_to_all(cut_along(shard, dim, count), axis, 0, 0, tiled=True)
    return jnp.sum(pieces, axis=0)


def one_axis_at_a_time(shard, axes):
    for axis in axes:
        shard = lax.psum(shard, axis)
    return shard


def primal_side(product, require_part, kind_part, dual_part):
    difference = require_part[None, :] - product
    residual = jnp.where(kind_part[None, :] == 1, jnp.maximum(difference, 0.0), difference)
    return (
        residual,
        jnp.sum(residual * residual, axis=1),
        jnp.sum(require_part * require_part),
        jnp.sum(require_part[None, :] * dual_part, axis=1),
    )


def dual_side(transposed, objective, lower_bound, upper_bound, variable_kind, primal_part):
    reduced = objective[None, :] - transposed
    lower_active = (variable_kind == 1) | (variable_kind == 3)
    upper_active = (variable_kind == 2) | (variable_kind == 3)
    multiplier = jnp.where(lower_active[None, :], jnp.maximum(reduced, 0.0), 0.0) + jnp.where(
        upper_active[None, :], jnp.minimum(reduced, 0.0), 0.0
    )
    residual = reduced - multiplier
    bound_sum = jnp.sum(
        lower_bound[None, :] * jnp.maximum(multiplier, 0.0)
        + upper_bound[None, :] * jnp.minimum(multiplier, 0.0),
        axis=1,
    )
    return (
        residual,
        jnp.sum(residual * residual, axis=1),
        jnp.sum(objective * objective),
        jnp.sum(objective[None, :] * primal_part, axis=1),
        bound_sum,
    )


def finish(
    primal_square,
    require_square,
    require_dot,
    dual_square,
    objective_square,
    objective_dot,
    bound_sum,
):
    primal_ratio = jnp.sqrt(primal_square) / (1.0 + jnp.sqrt(require_square))
    dual_ratio = jnp.sqrt(dual_square) / (1.0 + jnp.sqrt(objective_square))
    dual_value = require_dot + bound_sum
    duality_gap = jnp.abs(objective_dot - dual_value) / (
        1.0 + jnp.abs(objective_dot) + jnp.abs(dual_value)
    )
    return jnp.stack([primal_ratio, dual_ratio, duality_gap], axis=1)


def on_device(
    matrix_tiles,
    tile_rows,
    tile_columns,
    tile_counts,
    primal_iter,
    dual_iter,
    requirement,
    constraint_kind,
    objective,
    lower_bound,
    upper_bound,
    variable_kind,
):
    own_tiles = matrix_tiles[0, 0]
    slot_count = own_tiles.shape[0]
    block_size = own_tiles.shape[-1]
    candidates = primal_iter.shape[0]
    active = (lax.iota(jnp.int32, slot_count) < tile_counts[0, 0]).astype(jnp.float32)
    primal_group = collect(primal_iter, ROW, 1)
    dual_group = collect(dual_iter, COL, 1)
    column_blocks = primal_group.shape[1] // block_size
    row_blocks = dual_group.shape[1] // block_size
    column_pick = (
        tile_columns[0, 0][:, None] == lax.iota(jnp.int32, column_blocks)[None, :]
    ).astype(jnp.float32)
    column_pick = column_pick * active[:, None]
    row_pick = (tile_rows[0, 0][:, None] == lax.iota(jnp.int32, row_blocks)[None, :]).astype(
        jnp.float32
    )
    row_pick = row_pick * active[:, None]
    primal_pick = jnp.einsum(
        "tc,scb->stb",
        column_pick,
        primal_group.reshape(candidates, column_blocks, block_size),
        precision=HIGHEST_PRECISION,
    )
    dual_pick = jnp.einsum(
        "tr,srb->stb",
        row_pick,
        dual_group.reshape(candidates, row_blocks, block_size),
        precision=HIGHEST_PRECISION,
    )
    tile_product = jnp.einsum("tij,stj->tsi", own_tiles, primal_pick, precision=HIGHEST_PRECISION)
    tile_transposed = jnp.einsum("tij,sti->tsj", own_tiles, dual_pick, precision=HIGHEST_PRECISION)
    row_share = dual_iter.shape[1]
    column_share = primal_iter.shape[1]
    row_start = lax.axis_index(COL) * row_share
    column_start = lax.axis_index(ROW) * column_share
    product_part = jnp.einsum(
        "tr,tsi->sri", row_pick, tile_product, precision=HIGHEST_PRECISION
    ).reshape(candidates, row_blocks * block_size)
    transposed_part = jnp.einsum(
        "tc,tsj->scj", column_pick, tile_transposed, precision=HIGHEST_PRECISION
    ).reshape(candidates, column_blocks * block_size)
    product = sum_at_owner(product_part, COL, 1)
    transposed = sum_at_owner(transposed_part, ROW, 1)
    require_share = lax.dynamic_slice_in_dim(requirement, row_start, row_share)
    kind_share = lax.dynamic_slice_in_dim(constraint_kind, row_start, row_share)
    primal_residual, primal_square, require_square, require_dot = primal_side(
        product, require_share, kind_share, dual_iter
    )
    objective_share = lax.dynamic_slice_in_dim(objective, column_start, column_share)
    lower_share = lax.dynamic_slice_in_dim(lower_bound, column_start, column_share)
    upper_share = lax.dynamic_slice_in_dim(upper_bound, column_start, column_share)
    variable_share = lax.dynamic_slice_in_dim(variable_kind, column_start, column_share)
    dual_residual, dual_square, objective_square, objective_dot, bound_sum = dual_side(
        transposed, objective_share, lower_share, upper_share, variable_share, primal_iter
    )
    statistics = (
        primal_square,
        require_square,
        require_dot,
        dual_square,
        objective_square,
        objective_dot,
        bound_sum,
    )
    statistics = (
        one_axis_at_a_time(statistics[0], ROW_COL),
        one_axis_at_a_time(statistics[1], ROW_COL),
        one_axis_at_a_time(statistics[2], ROW_COL),
        one_axis_at_a_time(statistics[3], ROW_COL),
        one_axis_at_a_time(statistics[4], ROW_COL),
        one_axis_at_a_time(statistics[5], ROW_COL),
        one_axis_at_a_time(statistics[6], ROW_COL),
    )
    (
        primal_square,
        require_square,
        require_dot,
        dual_square,
        objective_square,
        objective_dot,
        bound_sum,
    ) = statistics
    metrics = finish(
        primal_square,
        require_square,
        require_dot,
        dual_square,
        objective_square,
        objective_dot,
        bound_sum,
    )
    return (primal_residual, dual_residual, metrics)


def solution(mesh):
    torus = Mesh(mesh.devices.reshape(4, 2, 2, 4, 2), ("row_0", "row_1", "col_0", "col_1", "col_2"))
    return jax.shard_map(
        on_device,
        mesh=torus,
        in_specs=(
            P(ROW, COL, None, None, None),
            P(ROW, COL, None),
            P(ROW, COL, None),
            P(ROW, COL),
            P(None, COL_ROW),
            P(None, ROW_COL),
            P(ROW),
            P(ROW),
            P(COL),
            P(COL),
            P(COL),
            P(COL),
        ),
        out_specs=(P(None, ROW_COL), P(None, COL_ROW), P()),
        check_vma=False,
    )
```

profile of v0, /device:TPU:1, one launch (start us, length us, event | category | flops | bytes accessed | tf_op | source)
XLA Modules:
  0.0 119.1 jit_solution(9777826574996980370)
XLA Ops:
  0.6 0.0 copy-start.2
  0.6 1.5 %broadcast_in_dim.44 = f32[8,2,4096]{2,1,0:T(2,128)} broadcast(f32[2,4096]{1,0:T(2,128)} %param.16), dimensions={1,2} | broadcast | bytes 294912 | tf_op jit(solution)/shard_map/broadcast_in_dim | solution.py:17
  2.2 8.5 %all-to-all-start = ((f32[8,2,4096]{2,1,0:T(2,128)}), f32[8,2,4096]{2,1,0:T(2,128)S(1)}, u32[]{:S(2)}, u32[]{:S(2)}) async-start(f32[8,2,4096]{2,1,0:T(2,128)} %broadcast_in_dim.44), calls=%async_computation | async-start | bytes 524288 | tf_op jit(solution)/shard_map/all_to_all | solution.py:18
  11.3 0.7 compare_or_fusion.1
  12.0 1.4 %multiply_reduce_fusion.4 = (f32[]{:T(128)}, f32[4096]{0:T(1024)S(1)}, f32[]{:T(128)}, f32[4096]{0:T(1024)S(1)}) fusion(f32[32768]{0:T(1024)} %param.20, s32[]{:T(128)} %select_n.23, f32[65536]{0:T(1024)} %param.18, s32[]{:T(128)S(6)} %select_n.21), kind=kLoop, calls=%fused_computation.21 | loop fusion | flops 16382 | bytes 65552 | tf_op jit(solution)/shard_map/reduce_sum | solution.py:77
  13.5 0.7 compare_or_fusion
  14.2 4.1 %all-to-all-done = f32[8,2,4096]{2,1,0:T(2,128)S(1)} async-done(((f32[8,2,4096]{2,1,0:T(2,128)}), f32[8,2,4096]{2,1,0:T(2,128)S(1)}, u32[]{:S(2)}, u32[]{:S(2)}) %all-to-all-start) | async-done | bytes 262176 | tf_op jit(solution)/shard_map/all_to_all | solution.py:18
  18.3 1.8 %broadcast_in_dim.45 = f32[16,2,4096]{2,1,0:T(2,128)} broadcast(f32[2,4096]{1,0:T(2,128)} %param.17), dimensions={1,2} | broadcast | bytes 557056 | tf_op jit(solution)/shard_map/broadcast_in_dim | solution.py:17
  20.1 6.5 %all-to-all-start.2 = ((f32[16,2,4096]{2,1,0:T(2,128)}), f32[16,2,4096]{2,1,0:T(2,128)S(1)}, u32[]{:S(2)}, u32[]{:S(2)}) async-start(f32[16,2,4096]{2,1,0:T(2,128)} %broadcast_in_dim.45), calls=%async_computation.2 | async-start | bytes 1048576 | tf_op jit(solution)/shard_map/all_to_all | solution.py:18
  26.6 0.2 copy.18
  26.7 0.1 reshape_reshape.12
  26.8 0.9 convolution_bitcast_fusion.2
  27.8 0.0 copy-start.3
  27.8 17.2 %fusion.2 = f32[16,2,512]{2,1,0:T(2,128)S(1)} fusion(f32[1,1,16,512,512]{4,3,2,1,0:T(8,128)} %param.12, f32[2,16,512]{2,1,0:T(8,128)S(1)} %convolution_bitcast_fusion.2), kind=kOutput, calls=%fused_computation.2 | convolution fusion | flops 100663296 | bytes 16908288 | tf_op jit(solution)/shard_map/tij,stj->tsi/dot_general | solution.py:144
  45.0 0.0 copy-start.1
  45.0 0.0 copy-start
  45.0 0.0 dynamic-slice-start
  45.0 0.0 dynamic-slice-start.1
  45.0 1.0 convolution_bitcast_fusion
  46.0 0.2 copy.21
  46.3 0.1 reshape_reshape.13
  46.4 1.2 %copy.22 = f32[16,2,4096]{2,1,0:T(2,128)} copy(f32[16,2,4096]{2,0,1:T(8,128)S(1)} %bitcast.42) | data formatting | bytes 1048576 | tf_op jit(solution)/shard_map/transpose | solution.py:35
  47.6 0.0 all-to-all-done.2
  47.6 5.7 %all-to-all-start.1 = ((f32[16,2,4096]{2,1,0:T(2,128)}), f32[16,2,4096]{2,1,0:T(2,128)S(1)}, u32[]{:S(2)}, u32[]{:S(2)}) async-start(f32[16,2,4096]{2,1,0:T(2,128)} %copy.22), calls=%async_computation.1 | async-start | bytes 1048576 | tf_op jit(solution)/shard_map/all_to_all | solution.py:40
  53.3 0.3 copy.23
  53.6 0.1 reshape_reshape.14
  53.7 0.4 convolution_bitcast_fusion.3
  54.1 11.5 %fusion = f32[16,2,512]{2,1,0:T(2,128)S(1)} fusion(f32[1,1,16,512,512]{4,3,2,1,0:T(8,128)} %param.12, f32[2,16,512]{2,1,0:T(8,128)S(1)} %convolution_bitcast_fusion.3), kind=kOutput, calls=%fused_computation | convolution fusion | flops 100663296 | bytes 16908288 | tf_op jit(solution)/shard_map/tij,sti->tsj/dot_general | solution.py:145
  65.6 0.5 convolution_bitcast_fusion.1
  66.1 0.1 reshape_reshape.15
  66.2 0.9 copy.37
  67.1 0.0 all-to-all-done.1
  67.1 3.4 %all-to-all-start.3 = ((f32[8,2,4096]{2,1,0:T(2,128)}), f32[8,2,4096]{2,1,0:T(2,128)S(1)}, u32[]{:S(2)}, u32[]{:S(2)}) async-start(f32[8,2,4096]{2,1,0:T(2,128)} %bitcast.39), calls=%async_computation.3 | async-start | bytes 524288 | tf_op jit(solution)/shard_map/all_to_all | solution.py:40
  70.5 0.7 dynamic-slice_compare_fusion
  71.2 0.2 reduce_sum.81
  71.4 0.8 multiply_reduce_fusion.3
  72.2 7.0 %all-to-all-done.3 = f32[8,2,4096]{2,1,0:T(2,128)S(1)} async-done(((f32[8,2,4096]{2,1,0:T(2,128)}), f32[8,2,4096]{2,1,0:T(2,128)S(1)}, u32[]{:S(2)}, u32[]{:S(2)}) %all-to-all-start.3) | async-done | bytes 262176 | tf_op jit(solution)/shard_map/all_to_all | solution.py:40
  79.2 0.1 reduce_sum.82
  79.3 0.0 copy-done
  79.3 0.0 dynamic-slice-done
  79.3 0.0 dynamic-slice-done.1
  79.3 0.9 multiply_reduce_fusion.1
  80.2 7.3 %all-reduce.1 = (f32[2]{0:T(128)S(1)}, f32[2]{0:T(128)S(1)}, f32[2]{0:T(128)S(1)}, f32[]{:T(128)}, f32[2]{0:T(128)S(1)}, /*index=5*/f32[]{:T(128)}) all-reduce(f32[2]{0:T(128)S(1)} %add.119, f32[2]{0:T(128)S(1)} %get-tuple-element.12, ...), channel_id=1, replica_groups=mesh['row_0'=4,'row_1'=2,'col_0'=2,'col_1'=4,'col_2'=2] {'row_0'}, use_global_device_ids=true, to_apply=%region_33.34 | all-reduce | flops 10 | bytes 80 | tf_op jit(solution)/shard_map/psum | solution.py:46
  87.5 5.9 %all-reduce.4 = (f32[2]{0:T(128)S(1)}, f32[2]{0:T(128)S(1)}, f32[2]{0:T(128)S(1)}, f32[]{:T(128)}, f32[2]{0:T(128)S(1)}, /*index=5*/f32[]{:T(128)}) all-reduce(f32[2]{0:T(128)S(1)} %get-tuple-element.20, f32[2]{0:T(128)S(1)} %get-tuple-element.21, ...), channel_id=1, replica_groups=mesh['row_0'=4,'row_1'=2,'col_0'=2,'col_1'=4,'col_2'=2] {'row_1'}, use_global_device_ids=true, to_apply=%region_34.35 | all-reduce | flops 10 | bytes 80 | tf_op jit(solution)/shard_map/psum | solution.py:46
  93.4 4.5 %all-reduce.3 = (f32[2]{0:T(128)S(1)}, f32[2]{0:T(128)S(1)}, f32[2]{0:T(128)S(1)}, f32[]{:T(128)}, f32[2]{0:T(128)S(1)}, /*index=5*/f32[]{:T(128)}) all-reduce(f32[2]{0:T(128)S(1)} %get-tuple-element.38, f32[2]{0:T(128)S(1)} %get-tuple-element.39, ...), channel_id=1, replica_groups=mesh['row_0'=4,'row_1'=2,'col_0'=2,'col_1'=4,'col_2'=2] {'col_0'}, use_global_device_ids=true, to_apply=%region_35.36 | all-reduce | flops 10 | bytes 80 | tf_op jit(solution)/shard_map/psum | solution.py:46
  97.9 8.7 %all-reduce = (f32[2]{0:T(128)S(1)}, f32[2]{0:T(128)S(1)}, f32[2]{0:T(128)S(1)}, f32[]{:T(128)}, f32[2]{0:T(128)S(1)}, /*index=5*/f32[]{:T(128)}) all-reduce(f32[2]{0:T(128)S(1)} %get-tuple-element.32, f32[2]{0:T(128)S(1)} %get-tuple-element.33, ...), channel_id=1, replica_groups=mesh['row_0'=4,'row_1'=2,'col_0'=2,'col_1'=4,'col_2'=2] {'col_1'}, use_global_device_ids=true, to_apply=%region_36.37 | all-reduce | flops 10 | bytes 80 | tf_op jit(solution)/shard_map/psum | solution.py:46
  106.6 10.4 %all-reduce.2 = (f32[2]{0:T(128)S(1)}, f32[2]{0:T(128)S(1)}, f32[2]{0:T(128)S(1)}, f32[]{:T(128)}, f32[2]{0:T(128)S(1)}, /*index=5*/f32[]{:T(128)}) all-reduce(f32[2]{0:T(128)S(1)} %get-tuple-element.14, f32[2]{0:T(128)S(1)} %get-tuple-element.15, ...), channel_id=1, replica_groups=mesh['row_0'=4,'row_1'=2,'col_0'=2,'col_1'=4,'col_2'=2] {'col_2'}, use_global_device_ids=true, to_apply=%region_37.38 | all-reduce | flops 10 | bytes 80 | tf_op jit(solution)/shard_map/psum | solution.py:46
  118.5 0.6 copy.27
  (9 shorter events, 0.1 us)
Async XLA Ops:
  0.6 44.4 %copy-start.2 = (s32[1,1,16]{2,1,0:T(1,128)S(1)}, s32[1,1,16]{2,1,0:T(1,128)}, u32[]{:S(2)}) copy-start(s32[1,1,16]{2,1,0:T(1,128)} %param.13) | copy-start | bytes 196
  2.2 16.1 %all-to-all-start = ((f32[8,2,4096]{2,1,0:T(2,128)}), f32[8,2,4096]{2,1,0:T(2,128)S(1)}, u32[]{:S(2)}, u32[]{:S(2)}) async-start(f32[8,2,4096]{2,1,0:T(2,128)} %broadcast_in_dim.44), calls=%async_computation | async-start | bytes 524288 | tf_op jit(solution)/shard_map/all_to_all | solution.py:18
  20.1 27.5 %all-to-all-start.2 = ((f32[16,2,4096]{2,1,0:T(2,128)}), f32[16,2,4096]{2,1,0:T(2,128)S(1)}, u32[]{:S(2)}, u32[]{:S(2)}) async-start(f32[16,2,4096]{2,1,0:T(2,128)} %broadcast_in_dim.45), calls=%async_computation.2 | async-start | bytes 1048576 | tf_op jit(solution)/shard_map/all_to_all | solution.py:18
  27.8 37.8 %copy-start.3 = (s32[1,1,16]{2,1,0:T(1,128)S(1)}, s32[1,1,16]{2,1,0:T(1,128)}, u32[]{:S(2)}) copy-start(s32[1,1,16]{2,1,0:T(1,128)} %param.14) | copy-start | bytes 196
  45.0 26.4 %copy-start.1 = (f32[2,4096]{1,0:T(2,128)S(1)}, f32[2,4096]{1,0:T(2,128)}, u32[]{:S(2)}) copy-start(f32[2,4096]{1,0:T(2,128)} %param.17) | copy-start | bytes 98308
  45.0 34.3 %copy-start = (f32[2,4096]{1,0:T(2,128)S(1)}, f32[2,4096]{1,0:T(2,128)}, u32[]{:S(2)}) copy-start(f32[2,4096]{1,0:T(2,128)} %param.16) | copy-start | bytes 98308
  45.0 34.3 %dynamic-slice-start = ((f32[32768]{0:T(1024)}, s32[]{:T(128)}), f32[4096]{0:T(1024)S(1)}, s32[]{:S(2)}) async-start(f32[32768]{0:T(1024)} %param.21, s32[]{:T(128)} %select_n.23), calls=%async_computation.4 | async-start | bytes 33280 | tf_op jit(solution)/shard_map/dynamic_slice | solution.py:164
  45.0 34.3 %dynamic-slice-start.1 = ((f32[32768]{0:T(1024)}, s32[]{:T(128)}), f32[4096]{0:T(1024)S(1)}, s32[]{:S(2)}) async-start(f32[32768]{0:T(1024)} %param.22, s32[]{:T(128)} %select_n.23), calls=%async_computation.5 | async-start | bytes 33280 | tf_op jit(solution)/shard_map/dynamic_slice | solution.py:165
  47.6 19.5 %all-to-all-start.1 = ((f32[16,2,4096]{2,1,0:T(2,128)}), f32[16,2,4096]{2,1,0:T(2,128)S(1)}, u32[]{:S(2)}, u32[]{:S(2)}) async-start(f32[16,2,4096]{2,1,0:T(2,128)} %copy.22), calls=%async_computation.1 | async-start | bytes 1048576 | tf_op jit(solution)/shard_map/all_to_all | solution.py:40
  67.1 12.1 %all-to-all-start.3 = ((f32[8,2,4096]{2,1,0:T(2,128)}), f32[8,2,4096]{2,1,0:T(2,128)S(1)}, u32[]{:S(2)}, u32[]{:S(2)}) async-start(f32[8,2,4096]{2,1,0:T(2,128)} %bitcast.39), calls=%async_computation.3 | async-start | bytes 524288 | tf_op jit(solution)/shard_map/all_to_all | solution.py:40
where the time goes:
time: 120 us; the launch traced here: 119 us
  blocking collectives  36.8 us (31%)
  matrix products  31.5 us (26%)
  starting transfers between devices  24.1 us (20%)
  waiting for transfers between devices  11.1 us (9%)
  local copies, waits for them, and re-layouts  7.04 us (6%)
  other arithmetic  5.56 us (5%)
  between operations  2.92 us (2%)
    psum x5, blocking collectives, one_axis_at_a_time(): shard = lax.psum(shard, axis)  36.8 us
    dot_general x1, matrix products, on_device(): jnp.einsum('tij,stj->tsi', own_tiles, primal_pick, precision=HIGHEST_PREC...  17.2 us
    all_to_all x2, starting transfers between devices, from_everyone(): return lax.all_to_all(copies, axis, split_axis=0, concat_axis=0, tiled=True)  15 us
    dot_general x1, matrix products, on_device(): jnp.einsum('tij,sti->tsj', own_tiles, dual_pick, precision=HIGHEST_PRECIS...  11.5 us
    all_to_all x2, starting transfers between devices, sum_at_owner(): lax.all_to_all(cut_along(shard, dim, count), axis, 0, 0, tiled=True)  9.13 us
    all_to_all x2, waiting for transfers between devices, sum_at_owner(): lax.all_to_all(cut_along(shard, dim, count), axis, 0, 0, tiled=True)  7 us
    all_to_all x2, waiting for transfers between devices, from_everyone(): return lax.all_to_all(copies, axis, split_axis=0, concat_axis=0, tiled=True)  4.11 us
    broadcast_in_dim x2, local copies, waits for them, and re-layouts, from_everyone(): copies = jnp.broadcast_to(shard, (lax.axis_size(axis), *shard.shape))  3.29 us
  transfers between devices with their start and end apart: 4, of which 2 were waited for; matrix products, arithmetic and copies ran while one was open for 33% of the time, Pallas kernels for 0%

commit v1 on v0

v1 whole, which is shorter than its diff:
```python
import functools

import jax
import jax.numpy as jnp
from jax import lax
from jax.experimental import pallas as pl
from jax.experimental.pallas import tpu as pltpu
from jax.sharding import Mesh
from jax.sharding import PartitionSpec as P

ROW = ("row_0", "row_1")
COL = ("col_0", "col_1", "col_2")
ROW_COL = ROW + COL
COL_ROW = COL + ROW
MESH_ID = pl.DeviceIdType.MESH

BLK = 512
SLOTS = 16
ROW_BLOCKS = 128
COL_BLOCKS = 64
OWN = 64

ROW_OFFS = [(dz, dy) for dz in range(4) for dy in range(2)]
COL_OFFS = [(dy, dx, dc) for dy in range(2) for dx in range(4) for dc in range(2)]
F32 = jnp.float32
BF16 = jnp.bfloat16


def split2(v):
    hi = v.astype(BF16)
    lo = (v - hi.astype(F32)).astype(BF16)
    return hi, lo


def spread(v):
    sub = lax.broadcasted_iota(jnp.int32, (8, 128), 0)
    hi = v.astype(BF16).astype(F32)
    lo = v - hi
    parts = []
    for k in range(4):
        keep = (sub // 2) == k
        parts.append(jnp.concatenate([jnp.where(keep, hi, 0.0), jnp.where(keep, lo, 0.0)], axis=0))
    return jnp.concatenate(parts, axis=1).astype(BF16)


def gathered(r):
    sub = lax.broadcasted_iota(jnp.int32, (8, 128), 0)
    out = jnp.zeros((8, 128), F32)
    for g in range(4):
        c = r[:8, 128 * g : 128 * g + 128] + r[8:, 128 * g : 128 * g + 128]
        c = c + pltpu.roll(c, 2, 0)
        c = c + pltpu.roll(c, 4, 0)
        out = jnp.where((sub // 2) == g, c, out)
    return out


def kernel(
    rows_ref,
    cols_ref,
    count_ref,
    tiles_ref,
    primal_ref,
    dual_ref,
    req_ref,
    ckind_ref,
    obj_ref,
    low_ref,
    up_ref,
    vkind_ref,
    pres_ref,
    dres_ref,
    met_ref,
    tiles,
    a_hi,
    a_lo,
    xg,
    yg,
    xo,
    yo,
    pbuf,
    part,
    tpart,
    precv,
    trecv,
    small,
    ismall,
    col_stat,
    row_stat,
    tile_sem,
    in_sem,
    row_send,
    row_recv,
    col_send,
    col_recv,
    prs_send,
    prs_recv,
    trs_send,
    trs_recv,
    cst_send,
    cst_recv,
    rst_send,
    rst_recv,
):
    z = lax.axis_index("row_0")
    yh = lax.axis_index("row_1")
    yl = lax.axis_index("col_0")
    x = lax.axis_index("col_1")
    core = lax.axis_index("col_2")
    r_me = z * 2 + yh
    c_me = (yl * 4 + x) * 2 + core

    def row_peer(off):
        pz, py = lax.rem(z + off[0], 4), lax.rem(yh + off[1], 2)
        return (pz, py, yl, x, core), pz * 2 + py

    def col_peer(off):
        py, px, pc = lax.rem(yl + off[0], 2), lax.rem(x + off[1], 4), lax.rem(core + off[2], 2)
        return (z, yh, py, px, pc), (py * 4 + px) * 2 + pc

    barrier = pltpu.get_barrier_semaphore()
    for off in ROW_OFFS[1:]:
        pl.semaphore_signal(barrier, inc=1, device_id=row_peer(off)[0], device_id_type=MESH_ID)
    for off in COL_OFFS[1:]:
        pl.semaphore_signal(barrier, inc=1, device_id=col_peer(off)[0], device_id_type=MESH_ID)

    own_x = pl.ds(r_me * 8, 8)
    own_y = pl.ds(c_me * 8, 8)
    cp_x = pltpu.make_async_copy(primal_ref.reshape(8, 8, 128), xg.at[own_x], in_sem.at[0])
    cp_y = pltpu.make_async_copy(dual_ref.reshape(8, 8, 128), yg.at[own_y], in_sem.at[1])
    cp_x.start()
    cp_y.start()
    own_copies = [
        pltpu.make_async_copy(primal_ref, xo, in_sem.at[8]),
        pltpu.make_async_copy(dual_ref, yo, in_sem.at[9]),
    ]
    mine_r = pl.ds(pl.multiple_of(c_me * 32, 32), 32)
    mine_c = pl.ds(pl.multiple_of(r_me * 32, 32), 32)
    extra = own_copies + [
        pltpu.make_async_copy(req_ref.at[mine_r], small.at[0], in_sem.at[2]),
        pltpu.make_async_copy(obj_ref.at[mine_c], small.at[1], in_sem.at[3]),
        pltpu.make_async_copy(low_ref.at[mine_c], small.at[2], in_sem.at[4]),
        pltpu.make_async_copy(up_ref.at[mine_c], small.at[3], in_sem.at[5]),
        pltpu.make_async_copy(ckind_ref.at[mine_r], ismall.at[0], in_sem.at[6]),
        pltpu.make_async_copy(vkind_ref.at[mine_c], ismall.at[1], in_sem.at[7]),
    ]
    for cp in extra:
        cp.start()

    def tile_copy(t):
        return pltpu.make_async_copy(tiles_ref.at[t], tiles.at[t], tile_sem.at[t])

    for t in range(SLOTS):
        tile_copy(t).start()

    cp_x.wait()
    cp_y.wait()
    pl.semaphore_wait(barrier, len(ROW_OFFS) + len(COL_OFFS) - 2)

    row_gather = []
    for i, off in enumerate(ROW_OFFS[1:]):
        row_gather.append(
            pltpu.make_async_remote_copy(
                src_ref=xg.at[own_x],
                dst_ref=xg.at[own_x],
                send_sem=row_send.at[i],
                recv_sem=row_recv.at[i],
                device_id=row_peer(off)[0],
                device_id_type=MESH_ID,
            )
        )
    col_gather = []
    for i, off in enumerate(COL_OFFS[1:]):
        col_gather.append(
            pltpu.make_async_remote_copy(
                src_ref=yg.at[own_y],
                dst_ref=yg.at[own_y],
                send_sem=col_send.at[i],
                recv_sem=col_recv.at[i],
                device_id=col_peer(off)[0],
                device_id_type=MESH_ID,
            )
        )
    for cp in row_gather:
        cp.start()
    for cp in col_gather:
        cp.start()

    lane = lax.broadcasted_iota(jnp.int32, (8, 128), 1)
    count = count_ref[0, 0]
    ridx = jnp.full((8, 128), -1, jnp.int32)
    cidx = jnp.full((8, 128), -1, jnp.int32)
    for t in range(SLOTS):
        here = (lax.rem(lane, SLOTS) == t) & (lane < 3 * SLOTS) & (jnp.full((8, 128), t, jnp.int32) < count)
        ridx = jnp.where(here, rows_ref[0, t], ridx)
        cidx = jnp.where(here, cols_ref[0, t], cidx)
    r_iota = lax.broadcasted_iota(jnp.int32, (ROW_BLOCKS, 128), 0)
    c_iota = lax.broadcasted_iota(jnp.int32, (COL_BLOCKS, 128), 0)
    r_hot = jnp.where(r_iota == ridx[:1], 1.0, 0.0).astype(BF16)[:, : 3 * SLOTS]
    c_hot = jnp.where(c_iota == cidx[:1], 1.0, 0.0).astype(BF16)[:, : 3 * SLOTS]

    def convert(t, carry):
        tile_copy(t).wait()

        def piece(i, c):
            sl = pl.ds(pl.multiple_of(i * 64, 64), 64)
            hi, lo = split2(tiles[t, sl, :])
            a_hi[t, sl, :] = hi
            a_lo[t, sl, :] = lo
            return c

        return lax.fori_loop(0, BLK // 64, piece, carry, unroll=True)

    lax.fori_loop(0, SLOTS, convert, 0)

    def scatter(hot, dest, blocks):
        cols = []
        for e in range(8):
            v = pbuf[pl.ds(e, SLOTS, stride=8), :]
            hi = v.astype(BF16)
            rest = v - hi.astype(F32)
            mid = rest.astype(BF16)
            lo = (rest - mid.astype(F32)).astype(BF16)
            cols.append(jnp.concatenate([hi, mid, lo], axis=0))
        rhs = jnp.concatenate(cols, axis=1)
        out = jnp.dot(hot, rhs, preferred_element_type=F32)
        for e in range(8):
            dest[pl.ds(e, blocks, stride=8), :] = out[:, e * 128 : (e + 1) * 128]

    for cp in row_gather:
        cp.wait_recv()

    def forward(t, carry):
        lhs = spread(xg[cols_ref[0, t]])
        dims = (((1,), (1,)), ((), ()))
        res = lax.dot_general(lhs, a_hi[t], dims, preferred_element_type=F32)
        res = res + lax.dot_general(lhs, a_lo[t], dims, preferred_element_type=F32)
        pbuf[pl.ds(pl.multiple_of(t * 8, 8), 8), :] = gathered(res)
        return carry

    lax.fori_loop(0, SLOTS, forward, 0)
    scatter(r_hot, part, ROW_BLOCKS)

    prs = []
    for i, off in enumerate(COL_OFFS[1:]):
        dev, idx = col_peer(off)
        prs.append(
            pltpu.make_async_remote_copy(
                src_ref=part.at[pl.ds(pl.multiple_of(idx * OWN, OWN), OWN)],
                dst_ref=precv.at[i],
                send_sem=prs_send.at[i],
                recv_sem=prs_recv.at[i],
                device_id=dev,
                device_id_type=MESH_ID,
            )
        )
    for cp in prs:
        cp.start()

    for cp in col_gather:
        cp.wait_recv()

    def backward(t, carry):
        lhs = spread(yg[rows_ref[0, t]])
        res = jnp.dot(lhs, a_hi[t], preferred_element_type=F32)
        res = res + jnp.dot(lhs, a_lo[t], preferred_element_type=F32)
        pbuf[pl.ds(pl.multiple_of(t * 8, 8), 8), :] = gathered(res)
        return carry

    lax.fori_loop(0, SLOTS, backward, 0)
    scatter(c_hot, tpart, COL_BLOCKS)

    trs = []
    for i, off in enumerate(ROW_OFFS[1:]):
        dev, idx = row_peer(off)
        trs.append(
            pltpu.make_async_remote_copy(
                src_ref=tpart.at[pl.ds(pl.multiple_of(idx * OWN, OWN), OWN)],
                dst_ref=trecv.at[i],
                send_sem=trs_send.at[i],
                recv_sem=trs_recv.at[i],
                device_id=dev,
                device_id_type=MESH_ID,
            )
        )
    for cp in trs:
        cp.start()

    for cp in extra:
        cp.wait()
    for cp in prs:
        cp.wait_recv()
    product = part[pl.ds(pl.multiple_of(c_me * OWN, OWN), OWN), :]
    for i in range(len(prs)):
        product = product + precv[i]
    pres_ref[...] = product
    sums = []
    req = small[0]
    is_ge = ismall[0] == 1
    dual_own = [yo[pl.ds(s, 32, stride=2), :] for s in range(2)]
    primal_own = [xo[pl.ds(s, 32, stride=2), :] for s in range(2)]
    stat_rows = [[], []]

    def total(v):
        return jnp.sum(v.reshape(4, 8, 128), axis=0)

    for s in range(2):
        diff = req - pres_ref[pl.ds(s, 32, stride=2), :]
        res = jnp.where(is_ge, jnp.maximum(diff, 0.0), diff)
        pres_ref[pl.ds(s, 32, stride=2), :] = res
        stat_rows[s] += [total(res * res), total(req * req), total(req * dual_own[s])]

    for cp in trs:
        cp.wait_recv()
    transposed = tpart[pl.ds(pl.multiple_of(r_me * OWN, OWN), OWN), :]
    for i in range(len(trs)):
        transposed = transposed + trecv[i]
    dres_ref[...] = transposed
    obj, low, up, vk = small[1], small[2], small[3], ismall[1]
    low_on = (vk == 1) | (vk == 3)
    up_on = (vk == 2) | (vk == 3)
    for s in range(2):
        reduced = obj - dres_ref[pl.ds(s, 32, stride=2), :]
        mult = jnp.where(low_on, jnp.maximum(reduced, 0.0), 0.0) + jnp.where(
            up_on, jnp.minimum(reduced, 0.0), 0.0
        )
        res = reduced - mult
        dres_ref[pl.ds(s, 32, stride=2), :] = res
        bound = low * jnp.maximum(mult, 0.0) + up * jnp.minimum(mult, 0.0)
        stat_rows[s] += [
            total(res * res),
            total(obj * obj),
            total(obj * primal_own[s]),
            total(bound),
        ]
    lane1 = lax.broadcasted_iota(jnp.int32, (1, 128), 1)
    for s in range(2):
        acc = jnp.zeros((1, 128), F32)
        for q in range(7):
            v = jnp.sum(stat_rows[s][q], axis=0, keepdims=True)
            v = jnp.sum(v, axis=1, keepdims=True)
            acc = jnp.where(lane1 == q, v, acc)
        col_stat[c_me, pl.ds(s, 1), :] = acc

    cst = []
    for i, off in enumerate(COL_OFFS[1:]):
        cst.append(
            pltpu.make_async_remote_copy(
                src_ref=col_stat.at[c_me],
                dst_ref=col_stat.at[c_me],
                send_sem=cst_send.at[i],
                recv_sem=cst_recv.at[i],
                device_id=col_peer(off)[0],
                device_id_type=MESH_ID,
            )
        )
    for cp in cst:
        cp.start()
    for cp in cst:
        cp.wait_recv()
    row_stat[r_me] = jnp.sum(col_stat[...], axis=0)
    rst = []
    for i, off in enumerate(ROW_OFFS[1:]):
        rst.append(
            pltpu.make_async_remote_copy(
                src_ref=row_stat.at[r_me],
                dst_ref=row_stat.at[r_me],
                send_sem=rst_send.at[i],
                recv_sem=rst_recv.at[i],
                device_id=row_peer(off)[0],
                device_id_type=MESH_ID,
            )
        )
    for cp in rst:
        cp.start()
    for cp in rst:
        cp.wait_recv()
    acc = jnp.sum(row_stat[...], axis=0)

    pick = [acc[:, q : q + 1] for q in range(7)]
    primal_square, require_square, require_dot = pick[0], pick[1], pick[2]
    dual_square, objective_square, objective_dot, bound_sum = pick[3], pick[4], pick[5], pick[6]
    primal_ratio = jnp.sqrt(primal_square) / (1.0 + jnp.sqrt(require_square))
    dual_ratio = jnp.sqrt(dual_square) / (1.0 + jnp.sqrt(objective_square))
    dual_value = require_dot + bound_sum
    gap = jnp.abs(objective_dot - dual_value) / (1.0 + jnp.abs(objective_dot) + jnp.abs(dual_value))
    lane2 = lax.broadcasted_iota(jnp.int32, (2, 128), 1)
    met = jnp.where(lane2 == 0, primal_ratio, jnp.where(lane2 == 1, dual_ratio, gap))
    met_ref[...] = met[:, :3]

    for group in (row_gather, col_gather, prs, trs, cst, rst):
        for cp in group:
            cp.wait_send()


def interleave(a):
    return a.reshape(2, 32, 128).transpose(1, 0, 2).reshape(OWN, 128)


def deinterleave(a):
    return a.reshape(32, 2, 128).transpose(1, 0, 2).reshape(2, 4096)


def on_device(
    matrix_tiles,
    tile_rows,
    tile_columns,
    tile_counts,
    primal_iter,
    dual_iter,
    requirement,
    constraint_kind,
    objective,
    lower_bound,
    upper_bound,
    variable_kind,
):
    hbm = pl.BlockSpec(memory_space=pl.ANY)
    smem = pl.BlockSpec(memory_space=pltpu.SMEM)
    vmem = pl.BlockSpec(memory_space=pltpu.VMEM)
    n_row, n_col = len(ROW_OFFS) - 1, len(COL_OFFS) - 1
    dma = pltpu.SemaphoreType.DMA
    pres, dres, metrics = pl.pallas_call(
        kernel,
        name="restart_check",
        out_shape=(
            jax.ShapeDtypeStruct((OWN, 128), F32),
            jax.ShapeDtypeStruct((OWN, 128), F32),
            jax.ShapeDtypeStruct((2, 3), F32),
        ),
        in_specs=[smem] * 3 + [hbm] * 9,
        out_specs=(vmem, vmem, vmem),
        scratch_shapes=[
            pltpu.VMEM((SLOTS, BLK, BLK), F32),
            pltpu.VMEM((SLOTS, BLK, BLK), BF16),
            pltpu.VMEM((SLOTS, BLK, BLK), BF16),
            pltpu.VMEM((COL_BLOCKS, 8, 128), F32),
            pltpu.VMEM((ROW_BLOCKS, 8, 128), F32),
            pltpu.VMEM((OWN, 128), F32),
            pltpu.VMEM((OWN, 128), F32),
            pltpu.VMEM((SLOTS * 8, 128), F32),
            pltpu.VMEM((16 * OWN, 128), F32),
            pltpu.VMEM((8 * OWN, 128), F32),
            pltpu.VMEM((n_col, OWN, 128), F32),
            pltpu.VMEM((n_row, OWN, 128), F32),
            pltpu.VMEM((4, 32, 128), F32),
            pltpu.VMEM((2, 32, 128), jnp.int32),
            pltpu.VMEM((n_col + 1, 2, 128), F32),
            pltpu.VMEM((n_row + 1, 2, 128), F32),
            dma((SLOTS,)),
            dma((10,)),
            dma((n_row,)),
            dma((n_row,)),
            dma((n_col,)),
            dma((n_col,)),
            dma((n_col,)),
            dma((n_col,)),
            dma((n_row,)),
            dma((n_row,)),
            dma((n_col,)),
            dma((n_col,)),
            dma((n_row,)),
            dma((n_row,)),
        ],
        compiler_params=pltpu.CompilerParams(
            collective_id=0, has_side_effects=True, vmem_limit_bytes=60 * 1024 * 1024
        ),
    )(
        tile_rows.reshape(1, SLOTS),
        tile_columns.reshape(1, SLOTS),
        tile_counts,
        matrix_tiles.reshape(SLOTS, BLK, BLK),
        interleave(primal_iter),
        interleave(dual_iter),
        requirement.reshape(512, 128),
        constraint_kind.reshape(512, 128),
        objective.reshape(256, 128),
        lower_bound.reshape(256, 128),
        upper_bound.reshape(256, 128),
        variable_kind.reshape(256, 128),
    )
    return deinterleave(pres), deinterleave(dres), metrics


def solution(mesh):
    torus = Mesh(mesh.devices.reshape(4, 2, 2, 4, 2), ROW_COL)
    return jax.shard_map(
        on_device,
        mesh=torus,
        in_specs=(
            P(ROW, COL, None, None, None),
            P(ROW, COL, None),
            P(ROW, COL, None),
            P(ROW, COL),
            P(None, COL_ROW),
            P(None, ROW_COL),
            P(ROW),
            P(ROW),
            P(COL),
            P(COL),
            P(COL),
            P(COL),
        ),
        out_specs=(P(None, ROW_COL), P(None, COL_ROW), P()),
        check_vma=False,
    )
```

time: 120 us -> 55.3 us (0.46)
  Pallas kernels: 0 us -> 49.8 us
  blocking collectives: 36.8 us -> 0 us
  matrix products: 31.5 us -> 0 us
  starting transfers between devices: 24.1 us -> 0 us
  waiting for transfers between devices: 11.1 us -> 0 us
  other arithmetic: 5.56 us -> 0 us
  local copies, waits for them, and re-layouts: 7.04 us -> 3.95 us
  between operations: 2.92 us -> 1.29 us
    pallas_call x0 -> x1, Pallas kernels: none -> 49.8 us  [on_device(): pl.pallas_call(kernel, name='restart_check', out_shape=(jax.ShapeDtypeStr...]
    psum x5 -> x0, blocking collectives: 36.8 us -> none  [one_axis_at_a_time(): shard = lax.psum(shard, axis)]
    dot_general x6 -> x0, matrix products: 31.5 us -> none  [the longest x1 17.2 us: on_device(): jnp.einsum('tij,stj->tsi', own_tiles, primal_pick, precision=HIGHEST_PREC...]
    all_to_all x4 -> x0, starting transfers between devices: 24.1 us -> none  [the longest x2 15 us: from_everyone(): return lax.all_to_all(copies, axis, split_axis=0, concat_axis=0, tiled=True)]
    all_to_all x4 -> x0, waiting for transfers between devices: 11.1 us -> none  [the longest x2 7 us: sum_at_owner(): lax.all_to_all(cut_along(shard, dim, count), axis, 0, 0, tiled=True)]
    reduce_sum x5 -> x0, other arithmetic: 3.33 us -> none  [the longest x1 1.42 us: dual_side(): jnp.sum(objective * objective)]
    broadcast_in_dim x2 -> x0, local copies, waits for them, and re-layouts: 3.29 us -> none  [from_everyone(): copies = jnp.broadcast_to(shard, (lax.axis_size(axis), *shard.shape))]
    unnamed x9 -> x3, local copies, waits for them, and re-layouts: 0.67 us -> 3.95 us
  transfers between devices with their start and end apart: 4 -> 0, of which waited for: 2 -> 0; matrix products, arithmetic and copies ran while one was open for 33% -> 0% of each run, Pallas kernels for 0% -> 0%
where the time goes in v1:
time: 55.3 us; the launch traced here: 55.1 us
  Pallas kernels  49.8 us (90%)
  local copies, waits for them, and re-layouts  3.95 us (7%)
  between operations  1.29 us (2%)
    pallas_call x1, Pallas kernels, on_device(): pl.pallas_call(kernel, name='restart_check', out_shape=(jax.ShapeDtypeStr...  49.8 us
    unnamed x3, local copies, waits for them, and re-layouts  3.95 us

profile of v1, /device:TPU:1, one launch (start us, length us, event | category | flops | bytes accessed | tf_op | source)
XLA Modules:
  0.0 55.1 jit_solution(12175620707108800950)
XLA Ops:
  1.3 49.8 %restart_check.1 = (f32[64,128]{1,0:T(8,128)}, f32[64,128]{1,0:T(8,128)}, f32[2,3]{1,0:T(2,128)}) custom-call(s32[1,16]{1,0:T(1,128)} %bitcast.40, s32[1,16]{1,0:T(1,128)} %bitcast.41, s32[1,1]{1,0:T(1,128)S(6)} %copy.22.count_ref, f32[16,512,512]{2,1,0:T(8,128)} %bitcast.29, f32[64,128]{1,0:T(8,128)} %bitcast.36, f32[64,128]{1,0:T(8,128)} %bitcast.37, ...), custom_call_target="tpu_custom_call" | custom-call | tf_op jit(solution)/shard_map/restart_check/pallas_call | solution.py:422
  51.1 1.4 %copy.23 = f32[2,4096]{1,0:T(2,128)} copy(f32[2,4096]{1,0:T(2,128)} %bitcast.39) | data formatting | bytes 65536
  52.5 1.4 %copy.24 = f32[2,4096]{1,0:T(2,128)} copy(f32[2,4096]{1,0:T(2,128)} %bitcast.38) | data formatting | bytes 65536
  53.9 1.2 %copy.25 = f32[2,3]{1,0:T(2,128)} copy(f32[2,3]{1,0:T(2,128)} %get-tuple-element.14) | data formatting | bytes 48

commit v2 on v1

v2 whole, which is shorter than its diff:
```python
import jax
import jax.numpy as jnp
from jax import lax
from jax.experimental import pallas as pl
from jax.experimental.pallas import tpu as pltpu
from jax.sharding import Mesh
from jax.sharding import PartitionSpec as P

ROW = ("row_0", "row_1")
COL = ("col_0", "col_1", "col_2")
ROW_COL = ROW + COL
COL_ROW = COL + ROW
MESH_ID = pl.DeviceIdType.MESH

BLK = 512
SLOTS = 16
ROW_BLOCKS = 128
COL_BLOCKS = 64
OWN = 64

CHIP_OFFS = [(1, 2), (1, 1), (1, 3), (0, 2), (1, 0), (0, 1), (0, 3), (0, 0)]
F32 = jnp.float32
BF16 = jnp.bfloat16


def split2(v):
    hi = v.astype(BF16)
    lo = (v - hi.astype(F32)).astype(BF16)
    return hi, lo


def spread(v):
    sub = lax.broadcasted_iota(jnp.int32, (8, 128), 0)
    hi = v.astype(BF16).astype(F32)
    lo = v - hi
    parts = []
    for k in range(4):
        keep = (sub // 2) == k
        parts.append(jnp.concatenate([jnp.where(keep, hi, 0.0), jnp.where(keep, lo, 0.0)], axis=0))
    return jnp.concatenate(parts, axis=1).astype(BF16)


def gathered(r):
    sub = lax.broadcasted_iota(jnp.int32, (8, 128), 0)
    out = jnp.zeros((8, 128), F32)
    for g in range(4):
        c = r[:8, 128 * g : 128 * g + 128] + r[8:, 128 * g : 128 * g + 128]
        c = c + pltpu.roll(c, 2, 0)
        c = c + pltpu.roll(c, 4, 0)
        out = jnp.where((sub // 2) == g, c, out)
    return out


def kernel(
    rows_ref,
    cols_ref,
    count_ref,
    tiles_ref,
    primal_ref,
    dual_ref,
    req_ref,
    ckind_ref,
    obj_ref,
    low_ref,
    up_ref,
    vkind_ref,
    pres_ref,
    dres_ref,
    met_ref,
    tiles,
    a_hi,
    a_lo,
    t_hi,
    t_lo,
    xg,
    yg,
    xo,
    yo,
    pbuf,
    part,
    tpart,
    drecv,
    precv,
    zrecv,
    zsum,
    yrecv,
    small,
    ismall,
    col_stat,
    row_stat,
    tile_sem,
    in_sem,
    gx_send,
    gx_recv,
    gy_send,
    gy_recv,
    gd_send,
    gd_recv,
    ds_send,
    ds_recv,
    ps_send,
    ps_recv,
    ts_send,
    ts_recv,
    st_send,
    st_recv,
):
    z = lax.axis_index("row_0")
    yh = lax.axis_index("row_1")
    yl = lax.axis_index("col_0")
    x = lax.axis_index("col_1")
    core = lax.axis_index("col_2")
    r_me = z * 2 + yh
    c_me = (yl * 4 + x) * 2 + core

    def up4(v, d):
        return lax.rem(v + d, 4)

    def z_dev(d):
        return (up4(z, d), yh, yl, x, core)

    def x_dev(d):
        return (z, yh, yl, up4(x, d), core)

    y_far = (z, 1 - yh, yl, x, core)
    y_near = (z, yh, 1 - yl, x, core)
    other = (z, yh, yl, x, 1 - core)

    barrier = pltpu.get_barrier_semaphore()
    near = [z_dev(d) for d in (2, 1, 3)] + [x_dev(d) for d in (2, 1, 3)] + [y_far, y_near, other]
    for dev in near:
        pl.semaphore_signal(barrier, inc=1, device_id=dev, device_id_type=MESH_ID)

    own_x = pl.ds(r_me * 8, 8)
    own_y = pl.ds(c_me * 8, 8)
    cp_x = pltpu.make_async_copy(primal_ref.reshape(8, 8, 128), xg.at[own_x], in_sem.at[0])
    cp_y = pltpu.make_async_copy(dual_ref.reshape(8, 8, 128), yg.at[own_y], in_sem.at[1])
    cp_x.start()
    cp_y.start()
    cp_x.wait()
    cp_y.wait()

    def tile_copy(t):
        return pltpu.make_async_copy(tiles_ref.at[t], tiles.at[t], tile_sem.at[t])

    for t in range(SLOTS):
        tile_copy(t).start()
    mine_r = pl.ds(pl.multiple_of(c_me * 32, 32), 32)
    mine_c = pl.ds(pl.multiple_of(r_me * 32, 32), 32)
    extra = [
        pltpu.make_async_copy(primal_ref, xo, in_sem.at[8]),
        pltpu.make_async_copy(dual_ref, yo, in_sem.at[9]),
        pltpu.make_async_copy(req_ref.at[mine_r], small.at[0], in_sem.at[2]),
        pltpu.make_async_copy(obj_ref.at[mine_c], small.at[1], in_sem.at[3]),
        pltpu.make_async_copy(low_ref.at[mine_c], small.at[2], in_sem.at[4]),
        pltpu.make_async_copy(up_ref.at[mine_c], small.at[3], in_sem.at[5]),
        pltpu.make_async_copy(ckind_ref.at[mine_r], ismall.at[0], in_sem.at[6]),
        pltpu.make_async_copy(vkind_ref.at[mine_c], ismall.at[1], in_sem.at[7]),
    ]
    for cp in extra:
        cp.start()

    lane = lax.broadcasted_iota(jnp.int32, (8, 128), 1)
    count = count_ref[0, 0]
    ridx = jnp.full((8, 128), -1, jnp.int32)
    cidx = jnp.full((8, 128), -1, jnp.int32)
    for t in range(SLOTS):
        here = (lax.rem(lane, SLOTS) == t) & (lane < 3 * SLOTS) & (jnp.full((8, 128), t, jnp.int32) < count)
        ridx = jnp.where(here, rows_ref[0, t], ridx)
        cidx = jnp.where(here, cols_ref[0, t], cidx)
    p_iota = lax.broadcasted_iota(jnp.int32, (ROW_BLOCKS, 128), 0)
    r_iota = ((p_iota // 8 % 8) * 2 + p_iota // 64) * 8 + p_iota % 8
    c_iota = lax.broadcasted_iota(jnp.int32, (COL_BLOCKS, 128), 0)
    r_hot = jnp.where(r_iota == ridx[:1], 1.0, 0.0).astype(BF16)[:, : 3 * SLOTS]
    c_hot = jnp.where(c_iota == cidx[:1], 1.0, 0.0).astype(BF16)[:, : 3 * SLOTS]

    pl.semaphore_wait(barrier, len(near))

    def send(src, dst, sems, i, dev):
        cp = pltpu.make_async_remote_copy(
            src_ref=src,
            dst_ref=dst,
            send_sem=sems[0].at[i],
            recv_sem=sems[1].at[i],
            device_id=dev,
            device_id_type=MESH_ID,
        )
        cp.start()
        return cp

    sent = []
    gx, gy, gd = (gx_send, gx_recv), (gy_send, gy_recv), (gd_send, gd_recv)

    def place(g, at, sems, i, dev):
        cp = send(g.at[pl.ds(at * 8, 8)], g.at[pl.ds(at * 8, 8)], sems, i, dev)
        sent.append(cp)
        return cp

    x_far = place(xg, r_me, gx, 0, y_far)
    x_z = [place(xg, r_me, gx, d, z_dev(d)) for d in (2, 1, 3)]
    y_n = place(yg, c_me, gy, 0, y_near)
    y_x = {d: place(yg, c_me, gy, d, x_dev(d)) for d in (2, 1, 3)}
    y_d = [place(yg, c_me, gd, 0, other)]

    def convert(t, carry):
        tile_copy(t).wait()

        def piece(i, c):
            sl = pl.ds(pl.multiple_of(i * 128, 128), 128)
            v = tiles[t, sl, :]
            hi, lo = split2(v)
            a_hi[t, sl, :] = hi
            a_lo[t, sl, :] = lo
            hi, lo = split2(v.T)
            t_hi[t, :, sl] = hi
            t_lo[t, :, sl] = lo
            return c

        return lax.fori_loop(0, BLK // 128, piece, carry, unroll=True)

    lax.fori_loop(0, 7, convert, 0)
    y_n.wait_recv()
    at = ((1 - yl) * 4 + x) * 2 + core
    y_x2 = {d: place(yg, at, gy, 3 + d, x_dev(d)) for d in (2, 1, 3)}
    y_d.append(place(yg, at, gd, 1, other))
    lax.fori_loop(7, 11, convert, 0)
    x_far.wait_recv()
    at = z * 2 + 1 - yh
    x_z2 = [place(xg, at, gx, 3 + d, z_dev(d)) for d in (2, 1, 3)]
    for d in (1, 3, 2):
        y_x[d].wait_recv()
        at = (yl * 4 + up4(x, 4 - d)) * 2 + core
        y_d.append(place(yg, at, gd, 1 + d, other))
    lax.fori_loop(11, 16, convert, 0)
    for d in (1, 3, 2):
        y_x2[d].wait_recv()
        at = ((1 - yl) * 4 + up4(x, 4 - d)) * 2 + core
        y_d.append(place(yg, at, gd, 4 + d, other))

    def scatter(hot, dest, blocks):
        cols = []
        for e in range(8):
            v = pbuf[pl.ds(e, SLOTS, stride=8), :]
            hi = v.astype(BF16)
            rest = v - hi.astype(F32)
            mid = rest.astype(BF16)
            lo = (rest - mid.astype(F32)).astype(BF16)
            cols.append(jnp.concatenate([hi, mid, lo], axis=0))
        rhs = jnp.concatenate(cols, axis=1)
        out = jnp.dot(hot, rhs, preferred_element_type=F32)
        for e in range(8):
            dest[pl.ds(e, blocks, stride=8), :] = out[:, e * 128 : (e + 1) * 128]

    def products(first, count, grouped, vec, index, hi_ref, lo_ref):
        def body(i, carry):
            for j in range(grouped):
                t = first + i * grouped + j
                lhs = spread(vec[index[0, t]])
                res = jnp.dot(lhs, hi_ref[t], preferred_element_type=F32)
                res = res + jnp.dot(lhs, lo_ref[t], preferred_element_type=F32)
                pbuf[pl.ds(pl.multiple_of(t * 8, 8), 8), :] = gathered(res)
            return carry

        lax.fori_loop(0, count // grouped, body, 0)

    dsem, psem, tsem, ssem = (ds_send, ds_recv), (ps_send, ps_recv), (ts_send, ts_recv), (st_send, st_recv)

    def z_rows(v):
        return pl.ds(pl.multiple_of(v * 2 * OWN, 2 * OWN), 2 * OWN)

    def share(c, off):
        chip = lax.rem(yl + off[0], 2) * 4 + up4(x, off[1])
        return pl.ds(pl.multiple_of((c * 8 + chip) * OWN, OWN), OWN)

    for cp in y_d:
        cp.wait_recv()
    products(0, SLOTS, 4, yg, rows_ref, a_hi, a_lo)
    scatter(c_hot, tpart, COL_BLOCKS)
    z_rs = []
    for i, d in enumerate((2, 1, 3)):
        z_rs.append(send(tpart.at[z_rows(up4(z, d))], zrecv.at[i], tsem, i, z_dev(d)))
    for cp in x_z + x_z2:
        cp.wait_recv()
    products(0, SLOTS, 4, xg, cols_ref, t_hi, t_lo)
    scatter(r_hot, part, ROW_BLOCKS)
    d_rs = []
    for i, off in enumerate(CHIP_OFFS):
        d_rs.append(send(part.at[share(1 - core, off)], drecv.at[i], dsem, i, other))
    p_rs = []
    for i, off in enumerate(CHIP_OFFS):
        d_rs[i].wait_recv()
        mine = share(core, off)
        part[mine, :] = part[mine, :] + drecv[i]
        if i < 7:
            dev = (z, yh, lax.rem(yl + off[0], 2), up4(x, off[1]), core)
            p_rs.append(send(part.at[mine], precv.at[i], psem, i, dev))
    for cp in extra:
        cp.wait()
    for cp in z_rs:
        cp.wait_recv()
    zsum[...] = tpart[z_rows(z), :] + zrecv[0] + zrecv[1] + zrecv[2]
    half = pl.ds(pl.multiple_of((1 - yh) * OWN, OWN), OWN)
    y_rs = send(zsum.at[half], yrecv, tsem, 3, y_far)
    dual_own = [yo[pl.ds(s, 32, stride=2), :] for s in range(2)]
    primal_own = [xo[pl.ds(s, 32, stride=2), :] for s in range(2)]
    stat_rows = [[], []]

    def total(v):
        return jnp.sum(v.reshape(4, 8, 128), axis=0)

    y_rs.wait_recv()
    dres_ref[...] = zsum[pl.ds(pl.multiple_of(yh * OWN, OWN), OWN), :] + yrecv[...]
    obj, low, up, vk = small[1], small[2], small[3], ismall[1]
    low_on = (vk == 1) | (vk == 3)
    up_on = (vk == 2) | (vk == 3)
    for s in range(2):
        reduced = obj - dres_ref[pl.ds(s, 32, stride=2), :]
        mult = jnp.where(low_on, jnp.maximum(reduced, 0.0), 0.0) + jnp.where(
            up_on, jnp.minimum(reduced, 0.0), 0.0
        )
        res = reduced - mult
        dres_ref[pl.ds(s, 32, stride=2), :] = res
        bound = low * jnp.maximum(mult, 0.0) + up * jnp.minimum(mult, 0.0)
        stat_rows[s] += [
            total(res * res),
            total(obj * obj),
            total(obj * primal_own[s]),
            total(bound),
        ]
    for cp in p_rs:
        cp.wait_recv()
    product = part[share(core, (0, 0)), :]
    for i in range(7):
        product = product + precv[i]
    pres_ref[...] = product
    req = small[0]
    is_ge = ismall[0] == 1
    for s in range(2):
        diff = req - pres_ref[pl.ds(s, 32, stride=2), :]
        res = jnp.where(is_ge, jnp.maximum(diff, 0.0), diff)
        pres_ref[pl.ds(s, 32, stride=2), :] = res
        stat_rows[s] += [total(res * res), total(req * req), total(req * dual_own[s])]

    lane1 = lax.broadcasted_iota(jnp.int32, (1, 128), 1)
    for s in range(2):
        acc = jnp.zeros((1, 128), F32)
        for q in range(7):
            v = jnp.sum(stat_rows[s][q], axis=0, keepdims=True)
            v = jnp.sum(v, axis=1, keepdims=True)
            acc = jnp.where(lane1 == q, v, acc)
        col_stat[c_me, pl.ds(s, 1), :] = acc

    stat = []
    for dy, dx in CHIP_OFFS:
        for dc in range(2):
            if (dy, dx, dc) != (0, 0, 0):
                dev = (z, yh, lax.rem(yl + dy, 2), up4(x, dx), lax.rem(core + dc, 2))
                stat.append(send(col_stat.at[c_me], col_stat.at[c_me], ssem, len(stat), dev))
    for cp in stat:
        cp.wait_recv()
    row_stat[r_me] = jnp.sum(col_stat[...], axis=0)
    rstat = []
    for d in (2, 1, 3, 0):
        for dy in (1, 0):
            if (d, dy) != (0, 0):
                dev = (up4(z, d), lax.rem(yh + dy, 2), yl, x, core)
                rstat.append(send(row_stat.at[r_me], row_stat.at[r_me], ssem, 15 + len(rstat), dev))
    for cp in rstat:
        cp.wait_recv()
    acc = jnp.sum(row_stat[...], axis=0)

    pick = [acc[:, q : q + 1] for q in range(7)]
    primal_square, require_square, require_dot = pick[4], pick[5], pick[6]
    dual_square, objective_square, objective_dot, bound_sum = pick[0], pick[1], pick[2], pick[3]
    primal_ratio = jnp.sqrt(primal_square) / (1.0 + jnp.sqrt(require_square))
    dual_ratio = jnp.sqrt(dual_square) / (1.0 + jnp.sqrt(objective_square))
    dual_value = require_dot + bound_sum
    gap = jnp.abs(objective_dot - dual_value) / (1.0 + jnp.abs(objective_dot) + jnp.abs(dual_value))
    lane2 = lax.broadcasted_iota(jnp.int32, (2, 128), 1)
    met = jnp.where(lane2 == 0, primal_ratio, jnp.where(lane2 == 1, dual_ratio, gap))
    met_ref[...] = met[:, :3]

    for cp in sent + d_rs + p_rs + z_rs + [y_rs] + stat + rstat:
        cp.wait_send()


def flush(a, b, c, a_out, b_out, c_out, sem):
    copies = [
        pltpu.make_async_copy(src, dst, sem.at[i])
        for i, (src, dst) in enumerate(((a, a_out), (b, b_out), (c, c_out)))
    ]
    for cp in copies:
        cp.start()
    for cp in copies:
        cp.wait()


def interleave(a):
    return a.reshape(2, 32, 128).transpose(1, 0, 2).reshape(OWN, 128)


def deinterleave(a):
    return a.reshape(32, 2, 128).transpose(1, 0, 2).reshape(2, 4096)


def on_device(
    matrix_tiles,
    tile_rows,
    tile_columns,
    tile_counts,
    primal_iter,
    dual_iter,
    requirement,
    constraint_kind,
    objective,
    lower_bound,
    upper_bound,
    variable_kind,
):
    hbm = pl.BlockSpec(memory_space=pl.ANY)
    smem = pl.BlockSpec(memory_space=pltpu.SMEM)
    vmem = pl.BlockSpec(memory_space=pltpu.VMEM)
    dma = pltpu.SemaphoreType.DMA
    pres, dres, metrics = pl.pallas_call(
        kernel,
        name="restart_check",
        out_shape=(
            pltpu.VMEM((OWN, 128), F32),
            pltpu.VMEM((OWN, 128), F32),
            pltpu.VMEM((2, 3), F32),
        ),
        in_specs=[smem] * 3 + [hbm] * 9,
        out_specs=(vmem, vmem, vmem),
        scratch_shapes=[
            pltpu.VMEM((SLOTS, BLK, BLK), F32),
            pltpu.VMEM((SLOTS, BLK, BLK), BF16),
            pltpu.VMEM((SLOTS, BLK, BLK), BF16),
            pltpu.VMEM((SLOTS, BLK, BLK), BF16),
            pltpu.VMEM((SLOTS, BLK, BLK), BF16),
            pltpu.VMEM((COL_BLOCKS, 8, 128), F32),
            pltpu.VMEM((ROW_BLOCKS, 8, 128), F32),
            pltpu.VMEM((OWN, 128), F32),
            pltpu.VMEM((OWN, 128), F32),
            pltpu.VMEM((SLOTS * 8, 128), F32),
            pltpu.VMEM((16 * OWN, 128), F32),
            pltpu.VMEM((8 * OWN, 128), F32),
            pltpu.VMEM((8, OWN, 128), F32),
            pltpu.VMEM((7, OWN, 128), F32),
            pltpu.VMEM((3, 2 * OWN, 128), F32),
            pltpu.VMEM((2 * OWN, 128), F32),
            pltpu.VMEM((OWN, 128), F32),
            pltpu.VMEM((4, 32, 128), F32),
            pltpu.VMEM((2, 32, 128), jnp.int32),
            pltpu.VMEM((16, 2, 128), F32),
            pltpu.VMEM((8, 2, 128), F32),
            dma((SLOTS,)),
            dma((10,)),
            dma((7,)),
            dma((7,)),
            dma((7,)),
            dma((7,)),
            dma((8,)),
            dma((8,)),
            dma((8,)),
            dma((8,)),
            dma((7,)),
            dma((7,)),
            dma((4,)),
            dma((4,)),
            dma((22,)),
            dma((22,)),
        ],
        compiler_params=pltpu.CompilerParams(
            collective_id=0, has_side_effects=True, vmem_limit_bytes=60 * 1024 * 1024
        ),
    )(
        tile_rows.reshape(1, SLOTS),
        tile_columns.reshape(1, SLOTS),
        tile_counts,
        matrix_tiles.reshape(SLOTS, BLK, BLK),
        interleave(primal_iter),
        interleave(dual_iter),
        requirement.reshape(512, 128),
        constraint_kind.reshape(512, 128),
        objective.reshape(256, 128),
        lower_bound.reshape(256, 128),
        upper_bound.reshape(256, 128),
        variable_kind.reshape(256, 128),
    )
    pres, dres, metrics = pl.pallas_call(
        flush,
        name="flush",
        out_shape=(
            pltpu.HBM((OWN, 128), F32),
            pltpu.HBM((OWN, 128), F32),
            pltpu.HBM((2, 3), F32),
        ),
        in_specs=[vmem] * 3,
        out_specs=(hbm,) * 3,
        scratch_shapes=[dma((3,))],
        compiler_params=pltpu.CompilerParams(vmem_limit_bytes=1024 * 1024),
    )(pres, dres, metrics)
    return deinterleave(pres), deinterleave(dres), metrics


def solution(mesh):
    torus = Mesh(mesh.devices.reshape(4, 2, 2, 4, 2), ROW_COL)
    return jax.shard_map(
        on_device,
        mesh=torus,
        in_specs=(
            P(ROW, COL, None, None, None),
            P(ROW, COL, None),
            P(ROW, COL, None),
            P(ROW, COL),
            P(None, COL_ROW),
            P(None, ROW_COL),
            P(ROW),
            P(ROW),
            P(COL),
            P(COL),
            P(COL),
            P(COL),
        ),
        out_specs=(P(None, ROW_COL), P(None, COL_ROW), P()),
        check_vma=False,
    )
```

time: 55.3 us -> 40.7 us (0.74)
  Pallas kernels: 49.8 us -> 39.2 us
  local copies, waits for them, and re-layouts: 3.95 us -> 0 us
    pallas_call x1 -> x2, Pallas kernels: 49.8 us -> 39.2 us  [the longest x1 38.6 us: on_device(): pl.pallas_call(kernel, name='restart_check', out_shape=(pltpu.VMEM((OWN,...]
    unnamed x3 -> x0, local copies, waits for them, and re-layouts: 3.95 us -> none
where the time goes in v2:
time: 40.7 us; the launch traced here: 40.5 us
  Pallas kernels  39.2 us (96%)
  between operations  1.29 us (3%)
    pallas_call x1, Pallas kernels, on_device(): pl.pallas_call(kernel, name='restart_check', out_shape=(pltpu.VMEM((OWN,...  38.6 us

profile of v2, /device:TPU:1, one launch (start us, length us, event | category | flops | bytes accessed | tf_op | source)
XLA Modules:
  0.0 40.5 jit_solution(16817064429667200901)
XLA Ops:
  1.3 38.6 %restart_check.1 = (f32[64,128]{1,0:T(8,128)S(1)}, f32[64,128]{1,0:T(8,128)S(1)}, f32[2,3]{1,0:T(2,128)S(1)}) custom-call(s32[1,16]{1,0:T(1,128)} %bitcast.38, s32[1,16]{1,0:T(1,128)} %bitcast.39, s32[1,1]{1,0:T(1,128)S(6)} %copy.19.count_ref, f32[16,512,512]{2,1,0:T(8,128)} %bitcast.29, f32[64,128]{1,0:T(8,128)} %bitcast.36, f32[64,128]{1,0:T(8,128)} %bitcast.37, ...), custom_call_target="tpu_custom_call" | custom-call | tf_op jit(solution)/shard_map/restart_check/pallas_call | solution.py:424
  39.9 0.7 %flush.1 = (f32[64,128]{1,0:T(8,128)}, f32[64,128]{1,0:T(8,128)}, f32[2,3]{1,0:T(2,128)}) custom-call(f32[64,128]{1,0:T(8,128)S(1)} %get-tuple-element.9.a, f32[64,128]{1,0:T(8,128)S(1)} %get-tuple-element.10.b, f32[2,3]{1,0:T(2,128)S(1)} %get-tuple-element.11.c), custom_call_target="tpu_custom_call" | custom-call | tf_op jit(solution)/shard_map/flush/pallas_call | solution.py:490

commit v3 on v2

--- a/solution.py
+++ b/solution.py
@@ -16,9 +16,28 @@
 SLOTS = 16
 ROW_BLOCKS = 128
 COL_BLOCKS = 64
+UNROLL = 16
 OWN = 64
 
 CHIP_OFFS = [(1, 2), (1, 1), (1, 3), (0, 2), (1, 0), (0, 1), (0, 3), (0, 0)]
+GROUPS = 4
+RECV = ["x_far", "x_z", "y_n", "y_x", "y_x2", "y_d", "z_rs", "y_rs", "p_rs", "stat"]
+
+
+def hops(off):
+    dz, dh, dl, dx, dc = off
+    return min(dz, 4 - dz) + min(dx, 4 - dx) + (2 * dh if not dl else 1) + 0.2 * dc
+
+
+PEERS = [
+    (dz, dh, dl, dx, dc)
+    for dz in range(4)
+    for dh in range(2)
+    for dl in range(2)
+    for dx in range(4)
+    for dc in range(2)
+]
+PEERS = sorted(PEERS[1:], key=hops, reverse=True)
 F32 = jnp.float32
 BF16 = jnp.bfloat16
 
@@ -52,9 +71,9 @@
 
 
 def kernel(
-    rows_ref,
-    cols_ref,
-    count_ref,
+    rows_hbm,
+    cols_hbm,
+    count_hbm,
     tiles_ref,
     primal_ref,
     dual_ref,
@@ -67,6 +86,8 @@
     pres_ref,
     dres_ref,
     met_ref,
+    tab,
+    count_ref,
     tiles,
     a_hi,
     a_lo,
@@ -74,8 +95,6 @@
     t_lo,
     xg,
     yg,
-    xo,
-    yo,
     pbuf,
     part,
     tpart,
@@ -86,24 +105,12 @@
     yrecv,
     small,
     ismall,
-    col_stat,
-    row_stat,
+    stats,
     tile_sem,
     in_sem,
-    gx_send,
-    gx_recv,
-    gy_send,
-    gy_recv,
-    gd_send,
-    gd_recv,
-    ds_send,
-    ds_recv,
-    ps_send,
-    ps_recv,
-    ts_send,
-    ts_recv,
-    st_send,
-    st_recv,
+    sent_sem,
+    recv_sem,
+    d_recv,
 ):
     z = lax.axis_index("row_0")
     yh = lax.axis_index("row_1")
@@ -126,6 +133,9 @@
     y_near = (z, yh, 1 - yl, x, core)
     other = (z, yh, yl, x, 1 - core)
 
+    def whole(ref, sem):
+        pltpu.make_async_copy(ref, ref, sem).wait()
+
     barrier = pltpu.get_barrier_semaphore()
     near = [z_dev(d) for d in (2, 1, 3)] + [x_dev(d) for d in (2, 1, 3)] + [y_far, y_near, other]
     for dev in near:
@@ -137,37 +147,45 @@
     cp_y = pltpu.make_async_copy(dual_ref.reshape(8, 8, 128), yg.at[own_y], in_sem.at[1])
     cp_x.start()
     cp_y.start()
+    tables = [
+        pltpu.make_async_copy(rows_hbm, tab.at[0], in_sem.at[4]),
+        pltpu.make_async_copy(cols_hbm, tab.at[1], in_sem.at[4]),
+        pltpu.make_async_copy(count_hbm, count_ref, in_sem.at[5]),
+    ]
+    for cp in tables:
+        cp.start()
     cp_x.wait()
     cp_y.wait()
 
-    def tile_copy(t):
-        return pltpu.make_async_copy(tiles_ref.at[t], tiles.at[t], tile_sem.at[t])
-
-    for t in range(SLOTS):
-        tile_copy(t).start()
+    def tile_copy(g):
+        four = pl.ds(g * (SLOTS // GROUPS), SLOTS // GROUPS)
+        return pltpu.make_async_copy(tiles_ref.at[four], tiles.at[four], tile_sem.at[g])
+
+    for g in range(GROUPS):
+        tile_copy(g).start()
     mine_r = pl.ds(pl.multiple_of(c_me * 32, 32), 32)
     mine_c = pl.ds(pl.multiple_of(r_me * 32, 32), 32)
     extra = [
-        pltpu.make_async_copy(primal_ref, xo, in_sem.at[8]),
-        pltpu.make_async_copy(dual_ref, yo, in_sem.at[9]),
         pltpu.make_async_copy(req_ref.at[mine_r], small.at[0], in_sem.at[2]),
-        pltpu.make_async_copy(obj_ref.at[mine_c], small.at[1], in_sem.at[3]),
-        pltpu.make_async_copy(low_ref.at[mine_c], small.at[2], in_sem.at[4]),
-        pltpu.make_async_copy(up_ref.at[mine_c], small.at[3], in_sem.at[5]),
-        pltpu.make_async_copy(ckind_ref.at[mine_r], ismall.at[0], in_sem.at[6]),
-        pltpu.make_async_copy(vkind_ref.at[mine_c], ismall.at[1], in_sem.at[7]),
+        pltpu.make_async_copy(obj_ref.at[mine_c], small.at[1], in_sem.at[2]),
+        pltpu.make_async_copy(low_ref.at[mine_c], small.at[2], in_sem.at[2]),
+        pltpu.make_async_copy(up_ref.at[mine_c], small.at[3], in_sem.at[2]),
+        pltpu.make_async_copy(ckind_ref.at[mine_r], ismall.at[0], in_sem.at[3]),
+        pltpu.make_async_copy(vkind_ref.at[mine_c], ismall.at[1], in_sem.at[3]),
     ]
     for cp in extra:
         cp.start()
 
+    whole(tab, in_sem.at[4])
+    tables[2].wait()
     lane = lax.broadcasted_iota(jnp.int32, (8, 128), 1)
     count = count_ref[0, 0]
     ridx = jnp.full((8, 128), -1, jnp.int32)
     cidx = jnp.full((8, 128), -1, jnp.int32)
     for t in range(SLOTS):
         here = (lax.rem(lane, SLOTS) == t) & (lane < 3 * SLOTS) & (jnp.full((8, 128), t, jnp.int32) < count)
-        ridx = jnp.where(here, rows_ref[0, t], ridx)
-        cidx = jnp.where(here, cols_ref[0, t], cidx)
+        ridx = jnp.where(here, tab[0, 0, t], ridx)
+        cidx = jnp.where(here, tab[1, 0, t], cidx)
     p_iota = lax.broadcasted_iota(jnp.int32, (ROW_BLOCKS, 128), 0)
     r_iota = ((p_iota // 8 % 8) * 2 + p_iota // 64) * 8 + p_iota % 8
     c_iota = lax.broadcasted_iota(jnp.int32, (COL_BLOCKS, 128), 0)
@@ -176,35 +194,33 @@
 
     pl.semaphore_wait(barrier, len(near))
 
-    def send(src, dst, sems, i, dev):
+    def send(src, dst, phase, recv, dev):
         cp = pltpu.make_async_remote_copy(
             src_ref=src,
             dst_ref=dst,
-            send_sem=sems[0].at[i],
-            recv_sem=sems[1].at[i],
+            send_sem=sent_sem.at[phase],
+            recv_sem=recv if not isinstance(recv, str) else recv_sem.at[RECV.index(recv)],
             device_id=dev,
             device_id_type=MESH_ID,
         )
         cp.start()
         return cp
 
-    sent = []
-    gx, gy, gd = (gx_send, gx_recv), (gy_send, gy_recv), (gd_send, gd_recv)
-
-    def place(g, at, sems, i, dev):
-        cp = send(g.at[pl.ds(at * 8, 8)], g.at[pl.ds(at * 8, 8)], sems, i, dev)
-        sent.append(cp)
-        return cp
-
-    x_far = place(xg, r_me, gx, 0, y_far)
-    x_z = [place(xg, r_me, gx, d, z_dev(d)) for d in (2, 1, 3)]
-    y_n = place(yg, c_me, gy, 0, y_near)
-    y_x = {d: place(yg, c_me, gy, d, x_dev(d)) for d in (2, 1, 3)}
-    y_d = [place(yg, c_me, gd, 0, other)]
+    def arrived(ref, name):
+        whole(ref, recv_sem.at[RECV.index(name)])
+
+    def place(g, at, recv, dev):
+        send(g.at[pl.ds(at * 8, 8)], g.at[pl.ds(at * 8, 8)], 0, recv, dev)
+
+    place(xg, r_me, "x_far", y_far)
+    for d in (2, 1, 3):
+        place(xg, r_me, "x_z", z_dev(d))
+    place(yg, c_me, "y_n", y_near)
+    for d in (2, 1, 3):
+        place(yg, c_me, "y_x", x_dev(d))
+    place(yg, c_me, "y_d", other)
 
     def convert(t, carry):
-        tile_copy(t).wait()
-
         def piece(i, c):
             sl = pl.ds(pl.multiple_of(i * 128, 128), 128)
             v = tiles[t, sl, :]
@@ -218,24 +234,28 @@
 
         return lax.fori_loop(0, BLK // 128, piece, carry, unroll=True)
 
-    lax.fori_loop(0, 7, convert, 0)
-    y_n.wait_recv()
+    tile_copy(0).wait()
+    lax.fori_loop(0, 4, convert, 0)
+    tile_copy(1).wait()
+    lax.fori_loop(4, 7, convert, 0)
+    arrived(yg.at[pl.ds(0, 8)], "y_n")
     at = ((1 - yl) * 4 + x) * 2 + core
-    y_x2 = {d: place(yg, at, gy, 3 + d, x_dev(d)) for d in (2, 1, 3)}
-    y_d.append(place(yg, at, gd, 1, other))
+    for d in (2, 1, 3):
+        place(yg, at, "y_x2", x_dev(d))
+    place(yg, at, "y_d", other)
+    tile_copy(2).wait()
     lax.fori_loop(7, 11, convert, 0)
-    x_far.wait_recv()
-    at = z * 2 + 1 - yh
-    x_z2 = [place(xg, at, gx, 3 + d, z_dev(d)) for d in (2, 1, 3)]
+    arrived(xg.at[pl.ds(0, 8)], "x_far")
+    for d in (2, 1, 3):
+        place(xg, z * 2 + 1 - yh, "x_z", z_dev(d))
+    arrived(yg.at[pl.ds(0, 24)], "y_x")
     for d in (1, 3, 2):
-        y_x[d].wait_recv()
-        at = (yl * 4 + up4(x, 4 - d)) * 2 + core
-        y_d.append(place(yg, at, gd, 1 + d, other))
+        place(yg, (yl * 4 + up4(x, d)) * 2 + core, "y_d", other)
+    tile_copy(3).wait()
     lax.fori_loop(11, 16, convert, 0)
+    arrived(yg.at[pl.ds(0, 24)], "y_x2")
     for d in (1, 3, 2):
-        y_x2[d].wait_recv()
-        at = ((1 - yl) * 4 + up4(x, 4 - d)) * 2 + core
-        y_d.append(place(yg, at, gd, 4 + d, other))
+        place(yg, ((1 - yl) * 4 + up4(x, d)) * 2 + core, "y_d", other)
 
     def scatter(hot, dest, blocks):
         cols = []
@@ -255,7 +275,7 @@
         def body(i, carry):
             for j in range(grouped):
                 t = first + i * grouped + j
-                lhs = spread(vec[index[0, t]])
+                lhs = spread(vec[tab[index, 0, t]])
                 res = jnp.dot(lhs, hi_ref[t], preferred_element_type=F32)
                 res = res + jnp.dot(lhs, lo_ref[t], preferred_element_type=F32)
                 pbuf[pl.ds(pl.multiple_of(t * 8, 8), 8), :] = gathered(res)
@@ -263,7 +283,6 @@
 
         lax.fori_loop(0, count // grouped, body, 0)
 
-    dsem, psem, tsem, ssem = (ds_send, ds_recv), (ps_send, ps_recv), (ts_send, ts_recv), (st_send, st_recv)
 
     def z_rows(v):
         return pl.ds(pl.multiple_of(v * 2 * OWN, 2 * OWN), 2 * OWN)
@@ -272,43 +291,38 @@
         chip = lax.rem(yl + off[0], 2) * 4 + up4(x, off[1])
         return pl.ds(pl.multiple_of((c * 8 + chip) * OWN, OWN), OWN)
 
-    for cp in y_d:
-        cp.wait_recv()
-    products(0, SLOTS, 4, yg, rows_ref, a_hi, a_lo)
+    arrived(yg.at[pl.ds(0, 64)], "y_d")
+    products(0, SLOTS, UNROLL, yg, 0, a_hi, a_lo)
     scatter(c_hot, tpart, COL_BLOCKS)
-    z_rs = []
     for i, d in enumerate((2, 1, 3)):
-        z_rs.append(send(tpart.at[z_rows(up4(z, d))], zrecv.at[i], tsem, i, z_dev(d)))
-    for cp in x_z + x_z2:
-        cp.wait_recv()
-    products(0, SLOTS, 4, xg, cols_ref, t_hi, t_lo)
+        send(tpart.at[z_rows(up4(z, d))], zrecv.at[i], 1, "z_rs", z_dev(d))
+    arrived(xg.at[pl.ds(0, 48)], "x_z")
+    products(0, SLOTS, UNROLL, xg, 1, t_hi, t_lo)
     scatter(r_hot, part, ROW_BLOCKS)
     d_rs = []
     for i, off in enumerate(CHIP_OFFS):
-        d_rs.append(send(part.at[share(1 - core, off)], drecv.at[i], dsem, i, other))
-    p_rs = []
+        d_rs.append(send(part.at[share(1 - core, off)], drecv.at[i], 1, d_recv.at[i], other))
     for i, off in enumerate(CHIP_OFFS):
         d_rs[i].wait_recv()
         mine = share(core, off)
         part[mine, :] = part[mine, :] + drecv[i]
         if i < 7:
             dev = (z, yh, lax.rem(yl + off[0], 2), up4(x, off[1]), core)
-            p_rs.append(send(part.at[mine], precv.at[i], psem, i, dev))
-    for cp in extra:
-        cp.wait()
-    for cp in z_rs:
-        cp.wait_recv()
+            send(part.at[mine], precv.at[i], 1, "p_rs", dev)
+    whole(small, in_sem.at[2])
+    whole(ismall, in_sem.at[3])
+    arrived(zrecv, "z_rs")
     zsum[...] = tpart[z_rows(z), :] + zrecv[0] + zrecv[1] + zrecv[2]
     half = pl.ds(pl.multiple_of((1 - yh) * OWN, OWN), OWN)
-    y_rs = send(zsum.at[half], yrecv, tsem, 3, y_far)
-    dual_own = [yo[pl.ds(s, 32, stride=2), :] for s in range(2)]
-    primal_own = [xo[pl.ds(s, 32, stride=2), :] for s in range(2)]
+    send(zsum.at[half], yrecv, 1, "y_rs", y_far)
+    dual_own = [yg.reshape(ROW_BLOCKS * 8, 128)[pl.ds(c_me * OWN + s, 32, stride=2), :] for s in range(2)]
+    primal_own = [xg.reshape(COL_BLOCKS * 8, 128)[pl.ds(r_me * OWN + s, 32, stride=2), :] for s in range(2)]
     stat_rows = [[], []]
 
     def total(v):
         return jnp.sum(v.reshape(4, 8, 128), axis=0)
 
-    y_rs.wait_recv()
+    arrived(yrecv, "y_rs")
     dres_ref[...] = zsum[pl.ds(pl.multiple_of(yh * OWN, OWN), OWN), :] + yrecv[...]
     obj, low, up, vk = small[1], small[2], small[3], ismall[1]
     low_on = (vk == 1) | (vk == 3)
@@ -327,8 +341,7 @@
             total(obj * primal_own[s]),
             total(bound),
         ]
-    for cp in p_rs:
-        cp.wait_recv()
+    arrived(precv, "p_rs")
     product = part[share(core, (0, 0)), :]
     for i in range(7):
         product = product + precv[i]
@@ -342,34 +355,21 @@
         stat_rows[s] += [total(res * res), total(req * req), total(req * dual_own[s])]
 
     lane1 = lax.broadcasted_iota(jnp.int32, (1, 128), 1)
+    acc = jnp.zeros((1, 128), F32)
     for s in range(2):
-        acc = jnp.zeros((1, 128), F32)
         for q in range(7):
             v = jnp.sum(stat_rows[s][q], axis=0, keepdims=True)
             v = jnp.sum(v, axis=1, keepdims=True)
-            acc = jnp.where(lane1 == q, v, acc)
-        col_stat[c_me, pl.ds(s, 1), :] = acc
-
-    stat = []
-    for dy, dx in CHIP_OFFS:
-        for dc in range(2):
-            if (dy, dx, dc) != (0, 0, 0):
-                dev = (z, yh, lax.rem(yl + dy, 2), up4(x, dx), lax.rem(core + dc, 2))
-                stat.append(send(col_stat.at[c_me], col_stat.at[c_me], ssem, len(stat), dev))
-    for cp in stat:
-        cp.wait_recv()
-    row_stat[r_me] = jnp.sum(col_stat[...], axis=0)
-    rstat = []
-    for d in (2, 1, 3, 0):
-        for dy in (1, 0):
-            if (d, dy) != (0, 0):
-                dev = (up4(z, d), lax.rem(yh + dy, 2), yl, x, core)
-                rstat.append(send(row_stat.at[r_me], row_stat.at[r_me], ssem, 15 + len(rstat), dev))
-    for cp in rstat:
-        cp.wait_recv()
-    acc = jnp.sum(row_stat[...], axis=0)
-
-    pick = [acc[:, q : q + 1] for q in range(7)]
+            acc = jnp.where(lane1 == 7 * s + q, v, acc)
+    me = r_me * 16 + c_me
+    stats[me] = acc
+    for dz, dh, dl, dx, dc in PEERS:
+        dev = (up4(z, dz), lax.rem(yh + dh, 2), lax.rem(yl + dl, 2), up4(x, dx), lax.rem(core + dc, 2))
+        send(stats.at[me], stats.at[me], 2, "stat", dev)
+    arrived(stats.at[pl.ds(0, 127)], "stat")
+    acc = jnp.sum(stats[...], axis=0)
+
+    pick = [jnp.concatenate([acc[:, q : q + 1], acc[:, 7 + q : 8 + q]], axis=0) for q in range(7)]
     primal_square, require_square, require_dot = pick[4], pick[5], pick[6]
     dual_square, objective_square, objective_dot, bound_sum = pick[0], pick[1], pick[2], pick[3]
     primal_ratio = jnp.sqrt(primal_square) / (1.0 + jnp.sqrt(require_square))
@@ -380,8 +380,9 @@
     met = jnp.where(lane2 == 0, primal_ratio, jnp.where(lane2 == 1, dual_ratio, gap))
     met_ref[...] = met[:, :3]
 
-    for cp in sent + d_rs + p_rs + z_rs + [y_rs] + stat + rstat:
-        cp.wait_send()
+    whole(tiles.at[0, pl.ds(0, 352)], sent_sem.at[0])
+    whole(tiles.at[0, pl.ds(0, 352)], sent_sem.at[1])
+    whole(stats.at[pl.ds(0, 127)], sent_sem.at[2])
 
 
 def flush(a, b, c, a_out, b_out, c_out, sem):
@@ -418,7 +419,6 @@
     variable_kind,
 ):
     hbm = pl.BlockSpec(memory_space=pl.ANY)
-    smem = pl.BlockSpec(memory_space=pltpu.SMEM)
     vmem = pl.BlockSpec(memory_space=pltpu.VMEM)
     dma = pltpu.SemaphoreType.DMA
     pres, dres, metrics = pl.pallas_call(
@@ -429,9 +429,11 @@
             pltpu.VMEM((OWN, 128), F32),
             pltpu.VMEM((2, 3), F32),
         ),
-        in_specs=[smem] * 3 + [hbm] * 9,
+        in_specs=[hbm] * 12,
         out_specs=(vmem, vmem, vmem),
         scratch_shapes=[
+            pltpu.SMEM((2, 1, SLOTS), jnp.int32),
+            pltpu.SMEM((1, 1), jnp.int32),
             pltpu.VMEM((SLOTS, BLK, BLK), F32),
             pltpu.VMEM((SLOTS, BLK, BLK), BF16),
             pltpu.VMEM((SLOTS, BLK, BLK), BF16),
@@ -439,8 +441,6 @@
             pltpu.VMEM((SLOTS, BLK, BLK), BF16),
             pltpu.VMEM((COL_BLOCKS, 8, 128), F32),
             pltpu.VMEM((ROW_BLOCKS, 8, 128), F32),
-            pltpu.VMEM((OWN, 128), F32),
-            pltpu.VMEM((OWN, 128), F32),
             pltpu.VMEM((SLOTS * 8, 128), F32),
             pltpu.VMEM((16 * OWN, 128), F32),
             pltpu.VMEM((8 * OWN, 128), F32),
@@ -451,24 +451,12 @@
             pltpu.VMEM((OWN, 128), F32),
             pltpu.VMEM((4, 32, 128), F32),
             pltpu.VMEM((2, 32, 128), jnp.int32),
-            pltpu.VMEM((16, 2, 128), F32),
-            pltpu.VMEM((8, 2, 128), F32),
-            dma((SLOTS,)),
-            dma((10,)),
-            dma((7,)),
-            dma((7,)),
-            dma((7,)),
-            dma((7,)),
+            pltpu.VMEM((128, 1, 128), F32),
+            dma((GROUPS,)),
+            dma((6,)),
+            dma((3,)),
+            dma((len(RECV),)),
             dma((8,)),
-            dma((8,)),
-            dma((8,)),
-            dma((8,)),
-            dma((7,)),
-            dma((7,)),
-            dma((4,)),
-            dma((4,)),
-            dma((22,)),
-            dma((22,)),
         ],
         compiler_params=pltpu.CompilerParams(
             collective_id=0, has_side_effects=True, vmem_limit_bytes=60 * 1024 * 1024

time: 40.7 us -> 36 us (0.88)
  Pallas kernels: 39.2 us -> 34.5 us
    pallas_call x1, Pallas kernels: 38.6 us -> 33.8 us  [on_device(): pl.pallas_call(kernel, name='restart_check', out_shape=(pltpu.VMEM((OWN,...]
where the time goes in v3:
time: 36 us; the launch traced here: 35.8 us
  Pallas kernels  34.5 us (96%)
  between operations  1.29 us (4%)
    pallas_call x1, Pallas kernels, on_device(): pl.pallas_call(kernel, name='restart_check', out_shape=(pltpu.VMEM((OWN,...  33.8 us

profile of v3, /device:TPU:1, one launch (start us, length us, event | category | flops | bytes accessed | tf_op | source)
XLA Modules:
  0.0 35.8 jit_solution(12130397100352765384)
XLA Ops:
  1.3 33.8 %restart_check.1 = (f32[64,128]{1,0:T(8,128)S(1)}, f32[64,128]{1,0:T(8,128)S(1)}, f32[2,3]{1,0:T(2,128)S(1)}) custom-call(s32[1,16]{1,0:T(1,128)} %bitcast.38, s32[1,16]{1,0:T(1,128)} %bitcast.39, s32[1,1]{1,0:T(1,128)S(6)} %copy.19.count_hbm, f32[16,512,512]{2,1,0:T(8,128)} %bitcast.29, f32[64,128]{1,0:T(8,128)} %bitcast.36, f32[64,128]{1,0:T(8,128)} %bitcast.37, ...), custom_call_target="tpu_custom_call" | custom-call | tf_op jit(solution)/shard_map/restart_check/pallas_call | solution.py:424
  35.1 0.7 %flush.1 = (f32[64,128]{1,0:T(8,128)}, f32[64,128]{1,0:T(8,128)}, f32[2,3]{1,0:T(2,128)}) custom-call(f32[64,128]{1,0:T(8,128)S(1)} %get-tuple-element.9.a, f32[64,128]{1,0:T(8,128)S(1)} %get-tuple-element.10.b, f32[2,3]{1,0:T(2,128)S(1)} %get-tuple-element.11.c), custom_call_target="tpu_custom_call" | custom-call | tf_op jit(solution)/shard_map/flush/pallas_call | solution.py:478

commit v4 on v3

--- a/solution.py
+++ b/solution.py
@@ -16,12 +16,14 @@
 SLOTS = 16
 ROW_BLOCKS = 128
 COL_BLOCKS = 64
-UNROLL = 16
+HALF = 512
 OWN = 64
 
 CHIP_OFFS = [(1, 2), (1, 1), (1, 3), (0, 2), (1, 0), (0, 1), (0, 3), (0, 0)]
-GROUPS = 4
-RECV = ["x_far", "x_z", "y_n", "y_x", "y_x2", "y_d", "z_rs", "y_rs", "p_rs", "stat"]
+VECTOR = [1, 3, 5, 7, 9, 11, 13]
+MATRIX = [t for t in range(SLOTS) if t not in VECTOR]
+BATCHES = [(0, 3), (3, 6), (6, 9), (9, 12), (12, 16)]
+RECV = ["x_far", "x_z", "y_n", "y_x", "y_x2", "y_d", "d_0", "d_1", "z_far", "z_near", "y_rs", "p_rs", "stat"]
 
 
 def hops(off):
@@ -59,11 +61,11 @@
     return jnp.concatenate(parts, axis=1).astype(BF16)
 
 
-def gathered(r):
+def gathered(r, groups):
     sub = lax.broadcasted_iota(jnp.int32, (8, 128), 0)
     out = jnp.zeros((8, 128), F32)
-    for g in range(4):
-        c = r[:8, 128 * g : 128 * g + 128] + r[8:, 128 * g : 128 * g + 128]
+    for i, g in enumerate(groups):
+        c = r[:8, 128 * i : 128 * i + 128] + r[8:, 128 * i : 128 * i + 128]
         c = c + pltpu.roll(c, 2, 0)
         c = c + pltpu.roll(c, 4, 0)
         out = jnp.where((sub // 2) == g, c, out)
@@ -93,6 +95,7 @@
     a_lo,
     t_hi,
     t_lo,
+    turned,
     xg,
     yg,
     pbuf,
@@ -100,6 +103,7 @@
     tpart,
     drecv,
     precv,
+    psum,
     zrecv,
     zsum,
     yrecv,
@@ -110,7 +114,6 @@
     in_sem,
     sent_sem,
     recv_sem,
-    d_recv,
 ):
     z = lax.axis_index("row_0")
     yh = lax.axis_index("row_1")
@@ -138,6 +141,7 @@
 
     barrier = pltpu.get_barrier_semaphore()
     near = [z_dev(d) for d in (2, 1, 3)] + [x_dev(d) for d in (2, 1, 3)] + [y_far, y_near, other]
+    near += [(z, yh, yl, up4(x, d), 1 - core) for d in (1, 3)] + [(z, yh, 1 - yl, x, 1 - core)]
     for dev in near:
         pl.semaphore_signal(barrier, inc=1, device_id=dev, device_id_type=MESH_ID)
 
@@ -158,10 +162,10 @@
     cp_y.wait()
 
     def tile_copy(g):
-        four = pl.ds(g * (SLOTS // GROUPS), SLOTS // GROUPS)
-        return pltpu.make_async_copy(tiles_ref.at[four], tiles.at[four], tile_sem.at[g])
-
-    for g in range(GROUPS):
+        some = pl.ds(BATCHES[g][0], BATCHES[g][1] - BATCHES[g][0])
+        return pltpu.make_async_copy(tiles_ref.at[some], tiles.at[some], tile_sem.at[g])
+
+    for g in range(len(BATCHES)):
         tile_copy(g).start()
     mine_r = pl.ds(pl.multiple_of(c_me * 32, 32), 32)
     mine_c = pl.ds(pl.multiple_of(r_me * 32, 32), 32)
@@ -216,50 +220,49 @@
     for d in (2, 1, 3):
         place(xg, r_me, "x_z", z_dev(d))
     place(yg, c_me, "y_n", y_near)
-    for d in (2, 1, 3):
+    place(yg, c_me, "y_x2", x_dev(2))
+    for d in (1, 3):
         place(yg, c_me, "y_x", x_dev(d))
     place(yg, c_me, "y_d", other)
 
-    def convert(t, carry):
-        def piece(i, c):
-            sl = pl.ds(pl.multiple_of(i * 128, 128), 128)
-            v = tiles[t, sl, :]
-            hi, lo = split2(v)
-            a_hi[t, sl, :] = hi
-            a_lo[t, sl, :] = lo
-            hi, lo = split2(v.T)
-            t_hi[t, :, sl] = hi
-            t_lo[t, :, sl] = lo
-            return c
-
-        return lax.fori_loop(0, BLK // 128, piece, carry, unroll=True)
-
-    tile_copy(0).wait()
-    lax.fori_loop(0, 4, convert, 0)
-    tile_copy(1).wait()
-    lax.fori_loop(4, 7, convert, 0)
+    def convert(g):
+        tile_copy(g).wait()
+        for t in range(*BATCHES[g]):
+            for i in range(BLK // 128):
+                sl = slice(i * 128, i * 128 + 128)
+                v = tiles[t, sl, :]
+                if t in VECTOR:
+                    turned[VECTOR.index(t), :, sl] = v.T
+                else:
+                    m = MATRIX.index(t)
+                    a_hi[m, sl, :], a_lo[m, sl, :] = split2(v)
+                    t_hi[m, :, sl], t_lo[m, :, sl] = split2(v.T)
+
+    for g in range(3):
+        convert(g)
     arrived(yg.at[pl.ds(0, 8)], "y_n")
     at = ((1 - yl) * 4 + x) * 2 + core
-    for d in (2, 1, 3):
-        place(yg, at, "y_x2", x_dev(d))
+    for c in (core, 1 - core):
+        for d in (1, 3):
+            place(yg, at, "y_d", (z, yh, yl, up4(x, d), c))
     place(yg, at, "y_d", other)
-    tile_copy(2).wait()
-    lax.fori_loop(7, 11, convert, 0)
+    convert(3)
+    arrived(yg.at[pl.ds(0, 8)], "y_x2")
+    at = (yl * 4 + up4(x, 2)) * 2 + core
+    for c in (core, 1 - core):
+        place(yg, at, "y_d", (z, yh, 1 - yl, x, c))
+    place(yg, at, "y_d", other)
     arrived(xg.at[pl.ds(0, 8)], "x_far")
     for d in (2, 1, 3):
         place(xg, z * 2 + 1 - yh, "x_z", z_dev(d))
-    arrived(yg.at[pl.ds(0, 24)], "y_x")
-    for d in (1, 3, 2):
+    arrived(yg.at[pl.ds(0, 16)], "y_x")
+    for d in (1, 3):
         place(yg, (yl * 4 + up4(x, d)) * 2 + core, "y_d", other)
-    tile_copy(3).wait()
-    lax.fori_loop(11, 16, convert, 0)
-    arrived(yg.at[pl.ds(0, 24)], "y_x2")
-    for d in (1, 3, 2):
-        place(yg, ((1 - yl) * 4 + up4(x, d)) * 2 + core, "y_d", other)
-
-    def scatter(hot, dest, blocks):
+    convert(4)
+
+    def scatter(hot, dest, blocks, base, rows):
         cols = []
-        for e in range(8):
+        for e in rows:
             v = pbuf[pl.ds(e, SLOTS, stride=8), :]
             hi = v.astype(BF16)
             rest = v - hi.astype(F32)
@@ -268,53 +271,71 @@
             cols.append(jnp.concatenate([hi, mid, lo], axis=0))
         rhs = jnp.concatenate(cols, axis=1)
         out = jnp.dot(hot, rhs, preferred_element_type=F32)
-        for e in range(8):
-            dest[pl.ds(e, blocks, stride=8), :] = out[:, e * 128 : (e + 1) * 128]
-
-    def products(first, count, grouped, vec, index, hi_ref, lo_ref):
-        def body(i, carry):
-            for j in range(grouped):
-                t = first + i * grouped + j
-                lhs = spread(vec[tab[index, 0, t]])
-                res = jnp.dot(lhs, hi_ref[t], preferred_element_type=F32)
-                res = res + jnp.dot(lhs, lo_ref[t], preferred_element_type=F32)
-                pbuf[pl.ds(pl.multiple_of(t * 8, 8), 8), :] = gathered(res)
-            return carry
-
-        lax.fori_loop(0, count // grouped, body, 0)
-
-
-    def z_rows(v):
-        return pl.ds(pl.multiple_of(v * 2 * OWN, 2 * OWN), 2 * OWN)
-
-    def share(c, off):
-        chip = lax.rem(yl + off[0], 2) * 4 + up4(x, off[1])
-        return pl.ds(pl.multiple_of((c * 8 + chip) * OWN, OWN), OWN)
-
-    arrived(yg.at[pl.ds(0, 64)], "y_d")
-    products(0, SLOTS, UNROLL, yg, 0, a_hi, a_lo)
-    scatter(c_hot, tpart, COL_BLOCKS)
-    for i, d in enumerate((2, 1, 3)):
-        send(tpart.at[z_rows(up4(z, d))], zrecv.at[i], 1, "z_rs", z_dev(d))
+        for i in range(len(rows)):
+            dest[pl.ds(base + i, blocks, stride=len(rows)), :] = out[:, i * 128 : (i + 1) * 128]
+
+    sub = lax.broadcasted_iota(jnp.int32, (8, 128), 0)
+
+    def vector_product(v, at, groups):
+        out = jnp.zeros((8, 128), F32)
+        for g in groups:
+            sums = [None, None]
+            for k in range(4):
+                block = at(slice(g * 128, g * 128 + 128), slice(k * 128, k * 128 + 128))
+                for s in range(2):
+                    term = block * v[2 * k + s : 2 * k + s + 1, :]
+                    sums[s] = term if sums[s] is None else sums[s] + term
+            for s in range(2):
+                out = jnp.where(sub == 2 * g + s, jnp.sum(sums[s].T, axis=0, keepdims=True), out)
+        return out
+
+    def products(vec, index, hi_ref, lo_ref, plain_ref, plain, groups):
+        lanes = slice(groups[0] * 128, groups[-1] * 128 + 128)
+        rows = slice(2 * groups[0], 2 * groups[-1] + 2)
+        for t in range(SLOTS):
+            v = vec[tab[index, 0, t]]
+            if t in VECTOR:
+                n = plain.index(t)
+                out = vector_product(v, lambda r, c, n=n: plain_ref[n, r, c], groups)
+            else:
+                m = MATRIX.index(t)
+                lhs = spread(v)
+                res = jnp.dot(lhs, hi_ref[m, :, lanes], preferred_element_type=F32)
+                res = res + jnp.dot(lhs, lo_ref[m, :, lanes], preferred_element_type=F32)
+                out = gathered(res, groups)
+            pbuf[8 * t + rows.start : 8 * t + rows.stop, :] = out[rows]
+
+    def own_rows(zz, hh):
+        return pl.ds(pl.multiple_of((zz * 2 + hh) * OWN, OWN), OWN)
+
+    def half_rows(h, c, chip, chips=1):
+        return pl.ds(pl.multiple_of(h * HALF + (c * 8 + chip) * 32, 32), chips * 32)
+
+    arrived(yg.at[pl.ds(0, 88)], "y_d")
+    products(yg, 0, a_hi, a_lo, turned, VECTOR, range(4))
+    scatter(c_hot, tpart, COL_BLOCKS, 0, range(8))
+    for w, hh in enumerate((1 - yh, yh)):
+        for i, d in enumerate((2, 1, 3)):
+            send(tpart.at[own_rows(up4(z, d), hh)], zrecv.at[w, i], 1, ("z_far", "z_near")[w], z_dev(d))
     arrived(xg.at[pl.ds(0, 48)], "x_z")
-    products(0, SLOTS, UNROLL, xg, 1, t_hi, t_lo)
-    scatter(r_hot, part, ROW_BLOCKS)
-    d_rs = []
-    for i, off in enumerate(CHIP_OFFS):
-        d_rs.append(send(part.at[share(1 - core, off)], drecv.at[i], 1, d_recv.at[i], other))
-    for i, off in enumerate(CHIP_OFFS):
-        d_rs[i].wait_recv()
-        mine = share(core, off)
-        part[mine, :] = part[mine, :] + drecv[i]
-        if i < 7:
-            dev = (z, yh, lax.rem(yl + off[0], 2), up4(x, off[1]), core)
-            send(part.at[mine], precv.at[i], 1, "p_rs", dev)
+    for h in range(2):
+        products(xg, 1, t_hi, t_lo, tiles, list(range(SLOTS)), range(2 * h, 2 * h + 2))
+        scatter(r_hot, part, ROW_BLOCKS, h * HALF, range(4 * h, 4 * h + 4))
+        send(part.at[half_rows(h, 1 - core, 0, 8)], drecv.at[h], 1, ("d_0", "d_1")[h], other)
+    for h in range(2):
+        arrived(drecv.at[h], ("d_0", "d_1")[h])
+        mine = half_rows(h, core, 0, 8)
+        part[mine, :] = part[mine, :] + drecv[h]
+        for i, off in enumerate(CHIP_OFFS[:-1]):
+            ny, nx = lax.rem(yl + off[0], 2), up4(x, off[1])
+            send(part.at[half_rows(h, core, ny * 4 + nx)], precv.at[i, pl.ds(32 * h, 32)], 1, "p_rs", (z, yh, ny, nx, core))
+    arrived(zrecv.at[0], "z_far")
+    zsum[...] = tpart[own_rows(z, 1 - yh), :] + zrecv[0, 0] + zrecv[0, 1] + zrecv[0, 2]
+    send(zsum, yrecv, 1, "y_rs", y_far)
     whole(small, in_sem.at[2])
     whole(ismall, in_sem.at[3])
-    arrived(zrecv, "z_rs")
-    zsum[...] = tpart[z_rows(z), :] + zrecv[0] + zrecv[1] + zrecv[2]
-    half = pl.ds(pl.multiple_of((1 - yh) * OWN, OWN), OWN)
-    send(zsum.at[half], yrecv, 1, "y_rs", y_far)
+    arrived(zrecv.at[1], "z_near")
+    near_sum = tpart[own_rows(z, yh), :] + zrecv[1, 0] + zrecv[1, 1] + zrecv[1, 2]
     dual_own = [yg.reshape(ROW_BLOCKS * 8, 128)[pl.ds(c_me * OWN + s, 32, stride=2), :] for s in range(2)]
     primal_own = [xg.reshape(COL_BLOCKS * 8, 128)[pl.ds(r_me * OWN + s, 32, stride=2), :] for s in range(2)]
     stat_rows = [[], []]
@@ -323,7 +344,7 @@
         return jnp.sum(v.reshape(4, 8, 128), axis=0)
 
     arrived(yrecv, "y_rs")
-    dres_ref[...] = zsum[pl.ds(pl.multiple_of(yh * OWN, OWN), OWN), :] + yrecv[...]
+    dres_ref[...] = near_sum + yrecv[...]
     obj, low, up, vk = small[1], small[2], small[3], ismall[1]
     low_on = (vk == 1) | (vk == 3)
     up_on = (vk == 2) | (vk == 3)
@@ -342,10 +363,14 @@
             total(bound),
         ]
     arrived(precv, "p_rs")
-    product = part[share(core, (0, 0)), :]
-    for i in range(7):
-        product = product + precv[i]
-    pres_ref[...] = product
+    for h in range(2):
+        product = part[half_rows(h, core, yl * 4 + x), :]
+        for i in range(7):
+            product = product + precv[i, 32 * h : 32 * h + 32, :]
+        psum[32 * h : 32 * h + 32, :] = product
+    for h in range(2):
+        for e in range(4):
+            pres_ref[pl.ds(4 * h + e, 8, stride=8), :] = psum[pl.ds(32 * h + e, 8, stride=4), :]
     req = small[0]
     is_ge = ismall[0] == 1
     for s in range(2):
@@ -435,28 +460,29 @@
             pltpu.SMEM((2, 1, SLOTS), jnp.int32),
             pltpu.SMEM((1, 1), jnp.int32),
             pltpu.VMEM((SLOTS, BLK, BLK), F32),
-            pltpu.VMEM((SLOTS, BLK, BLK), BF16),
-            pltpu.VMEM((SLOTS, BLK, BLK), BF16),
-            pltpu.VMEM((SLOTS, BLK, BLK), BF16),
-            pltpu.VMEM((SLOTS, BLK, BLK), BF16),
+            pltpu.VMEM((len(MATRIX), BLK, BLK), BF16),
+            pltpu.VMEM((len(MATRIX), BLK, BLK), BF16),
+            pltpu.VMEM((len(MATRIX), BLK, BLK), BF16),
+            pltpu.VMEM((len(MATRIX), BLK, BLK), BF16),
+            pltpu.VMEM((len(VECTOR), BLK, BLK), F32),
             pltpu.VMEM((COL_BLOCKS, 8, 128), F32),
             pltpu.VMEM((ROW_BLOCKS, 8, 128), F32),
             pltpu.VMEM((SLOTS * 8, 128), F32),
             pltpu.VMEM((16 * OWN, 128), F32),
             pltpu.VMEM((8 * OWN, 128), F32),
-            pltpu.VMEM((8, OWN, 128), F32),
+            pltpu.VMEM((2, HALF // 2, 128), F32),
             pltpu.VMEM((7, OWN, 128), F32),
-            pltpu.VMEM((3, 2 * OWN, 128), F32),
-            pltpu.VMEM((2 * OWN, 128), F32),
+            pltpu.VMEM((OWN, 128), F32),
+            pltpu.VMEM((2, 3, OWN, 128), F32),
+            pltpu.VMEM((OWN, 128), F32),
             pltpu.VMEM((OWN, 128), F32),
             pltpu.VMEM((4, 32, 128), F32),
             pltpu.VMEM((2, 32, 128), jnp.int32),
             pltpu.VMEM((128, 1, 128), F32),
-            dma((GROUPS,)),
+            dma((len(BATCHES),)),
             dma((6,)),
             dma((3,)),
             dma((len(RECV),)),
-            dma((8,)),
         ],
         compiler_params=pltpu.CompilerParams(
             collective_id=0, has_side_effects=True, vmem_limit_bytes=60 * 1024 * 1024

time: 36 us -> 34 us (0.944)
  Pallas kernels: 34.5 us -> 32.5 us
    pallas_call x1, Pallas kernels: 33.8 us -> 31.8 us  [on_device(): pl.pallas_call(kernel, name='restart_check', out_shape=(pltpu.VMEM((OWN,...]
where the time goes in v4:
time: 34 us; the launch traced here: 33.8 us
  Pallas kernels  32.5 us (96%)
  between operations  1.29 us (4%)
    pallas_call x1, Pallas kernels, on_device(): pl.pallas_call(kernel, name='restart_check', out_shape=(pltpu.VMEM((OWN,...  31.8 us

profile of v4, /device:TPU:1, one launch (start us, length us, event | category | flops | bytes accessed | tf_op | source)
XLA Modules:
  0.0 33.8 jit_solution(2258716539801884207)
XLA Ops:
  1.3 31.8 %restart_check.1 = (f32[64,128]{1,0:T(8,128)S(1)}, f32[64,128]{1,0:T(8,128)S(1)}, f32[2,3]{1,0:T(2,128)S(1)}) custom-call(s32[1,16]{1,0:T(1,128)} %bitcast.38, s32[1,16]{1,0:T(1,128)} %bitcast.39, s32[1,1]{1,0:T(1,128)S(6)} %copy.19.count_hbm, f32[16,512,512]{2,1,0:T(8,128)} %bitcast.29, f32[64,128]{1,0:T(8,128)} %bitcast.36, f32[64,128]{1,0:T(8,128)} %bitcast.37, ...), custom_call_target="tpu_custom_call" | custom-call | tf_op jit(solution)/shard_map/restart_check/pallas_call | solution.py:449
  33.1 0.7 %flush.1 = (f32[64,128]{1,0:T(8,128)}, f32[64,128]{1,0:T(8,128)}, f32[2,3]{1,0:T(2,128)}) custom-call(f32[64,128]{1,0:T(8,128)S(1)} %get-tuple-element.9.a, f32[64,128]{1,0:T(8,128)S(1)} %get-tuple-element.10.b, f32[2,3]{1,0:T(2,128)S(1)} %get-tuple-element.11.c), custom_call_target="tpu_custom_call" | custom-call | tf_op jit(solution)/shard_map/flush/pallas_call | solution.py:504

commit v5 on v4

--- a/solution.py
+++ b/solution.py
@@ -20,7 +20,7 @@
 OWN = 64
 
 CHIP_OFFS = [(1, 2), (1, 1), (1, 3), (0, 2), (1, 0), (0, 1), (0, 3), (0, 0)]
-VECTOR = [1, 3, 5, 7, 9, 11, 13]
+VECTOR = [1, 3, 5, 7, 9, 11, 13, 15]
 MATRIX = [t for t in range(SLOTS) if t not in VECTOR]
 BATCHES = [(0, 3), (3, 6), (6, 9), (9, 12), (12, 16)]
 RECV = ["x_far", "x_z", "y_n", "y_x", "y_x2", "y_d", "d_0", "d_1", "z_far", "z_near", "y_rs", "p_rs", "stat"]
@@ -216,18 +216,20 @@
     def place(g, at, recv, dev):
         send(g.at[pl.ds(at * 8, 8)], g.at[pl.ds(at * 8, 8)], 0, recv, dev)
 
+    place(yg, c_me, "y_n", y_near)
     place(xg, r_me, "x_far", y_far)
+    place(yg, c_me, "y_x2", x_dev(2))
     for d in (2, 1, 3):
         place(xg, r_me, "x_z", z_dev(d))
-    place(yg, c_me, "y_n", y_near)
-    place(yg, c_me, "y_x2", x_dev(2))
     for d in (1, 3):
         place(yg, c_me, "y_x", x_dev(d))
     place(yg, c_me, "y_d", other)
 
-    def convert(g):
-        tile_copy(g).wait()
-        for t in range(*BATCHES[g]):
+    def convert(*which):
+        for t in which:
+            for g, (begin, _) in enumerate(BATCHES):
+                if t == begin:
+                    tile_copy(g).wait()
             for i in range(BLK // 128):
                 sl = slice(i * 128, i * 128 + 128)
                 v = tiles[t, sl, :]
@@ -238,27 +240,27 @@
                     a_hi[m, sl, :], a_lo[m, sl, :] = split2(v)
                     t_hi[m, :, sl], t_lo[m, :, sl] = split2(v.T)
 
-    for g in range(3):
-        convert(g)
+    convert(*range(6))
     arrived(yg.at[pl.ds(0, 8)], "y_n")
     at = ((1 - yl) * 4 + x) * 2 + core
     for c in (core, 1 - core):
         for d in (1, 3):
             place(yg, at, "y_d", (z, yh, yl, up4(x, d), c))
     place(yg, at, "y_d", other)
-    convert(3)
+    convert(6, 7, 8)
     arrived(yg.at[pl.ds(0, 8)], "y_x2")
     at = (yl * 4 + up4(x, 2)) * 2 + core
     for c in (core, 1 - core):
         place(yg, at, "y_d", (z, yh, 1 - yl, x, c))
     place(yg, at, "y_d", other)
+    convert(9)
     arrived(xg.at[pl.ds(0, 8)], "x_far")
     for d in (2, 1, 3):
         place(xg, z * 2 + 1 - yh, "x_z", z_dev(d))
     arrived(yg.at[pl.ds(0, 16)], "y_x")
     for d in (1, 3):
         place(yg, (yl * 4 + up4(x, d)) * 2 + core, "y_d", other)
-    convert(4)
+    convert(*range(10, SLOTS))
 
     def scatter(hot, dest, blocks, base, rows):
         cols = []
@@ -322,16 +324,22 @@
         products(xg, 1, t_hi, t_lo, tiles, list(range(SLOTS)), range(2 * h, 2 * h + 2))
         scatter(r_hot, part, ROW_BLOCKS, h * HALF, range(4 * h, 4 * h + 4))
         send(part.at[half_rows(h, 1 - core, 0, 8)], drecv.at[h], 1, ("d_0", "d_1")[h], other)
+    def hand_out(h, steps):
+        for i, off in enumerate(CHIP_OFFS[:-1]):
+            if off[0] in steps:
+                ny, nx = lax.rem(yl + off[0], 2), up4(x, off[1])
+                dev = (z, yh, ny, nx, core)
+                send(part.at[half_rows(h, core, ny * 4 + nx)], precv.at[i, pl.ds(32 * h, 32)], 1, "p_rs", dev)
+
     for h in range(2):
         arrived(drecv.at[h], ("d_0", "d_1")[h])
         mine = half_rows(h, core, 0, 8)
         part[mine, :] = part[mine, :] + drecv[h]
-        for i, off in enumerate(CHIP_OFFS[:-1]):
-            ny, nx = lax.rem(yl + off[0], 2), up4(x, off[1])
-            send(part.at[half_rows(h, core, ny * 4 + nx)], precv.at[i, pl.ds(32 * h, 32)], 1, "p_rs", (z, yh, ny, nx, core))
+        hand_out(h, (0, 1) if h == 0 else (0,))
     arrived(zrecv.at[0], "z_far")
     zsum[...] = tpart[own_rows(z, 1 - yh), :] + zrecv[0, 0] + zrecv[0, 1] + zrecv[0, 2]
     send(zsum, yrecv, 1, "y_rs", y_far)
+    hand_out(1, (1,))
     whole(small, in_sem.at[2])
     whole(ismall, in_sem.at[3])
     arrived(zrecv.at[1], "z_near")
@@ -342,6 +350,16 @@
 
     def total(v):
         return jnp.sum(v.reshape(4, 8, 128), axis=0)
+
+    lane1 = lax.broadcasted_iota(jnp.int32, (1, 128), 1)
+
+    def lane_sums(acc, begin, end):
+        for s in range(2):
+            for q in range(begin, end):
+                v = jnp.sum(stat_rows[s][q], axis=0, keepdims=True)
+                v = jnp.sum(v, axis=1, keepdims=True)
+                acc = jnp.where(lane1 == 7 * s + q, v, acc)
+        return acc
 
     arrived(yrecv, "y_rs")
     dres_ref[...] = near_sum + yrecv[...]
@@ -362,6 +380,7 @@
             total(obj * primal_own[s]),
             total(bound),
         ]
+    acc = lane_sums(jnp.zeros((1, 128), F32), 0, 4)
     arrived(precv, "p_rs")
     for h in range(2):
         product = part[half_rows(h, core, yl * 4 + x), :]
@@ -379,15 +398,8 @@
         pres_ref[pl.ds(s, 32, stride=2), :] = res
         stat_rows[s] += [total(res * res), total(req * req), total(req * dual_own[s])]
 
-    lane1 = lax.broadcasted_iota(jnp.int32, (1, 128), 1)
-    acc = jnp.zeros((1, 128), F32)
-    for s in range(2):
-        for q in range(7):
-            v = jnp.sum(stat_rows[s][q], axis=0, keepdims=True)
-            v = jnp.sum(v, axis=1, keepdims=True)
-            acc = jnp.where(lane1 == 7 * s + q, v, acc)
     me = r_me * 16 + c_me
-    stats[me] = acc
+    stats[me] = lane_sums(acc, 4, 7)
     for dz, dh, dl, dx, dc in PEERS:
         dev = (up4(z, dz), lax.rem(yh + dh, 2), lax.rem(yl + dl, 2), up4(x, dx), lax.rem(core + dc, 2))
         send(stats.at[me], stats.at[me], 2, "stat", dev)

time: 34 us -> 33.4 us (0.982)
  Pallas kernels: 32.5 us -> 31.9 us
    pallas_call x1, Pallas kernels: 31.8 us -> 31.2 us  [on_device(): pl.pallas_call(kernel, name='restart_check', out_shape=(pltpu.VMEM((OWN,...]
where the time goes in v5:
time: 33.4 us; the launch traced here: 33.2 us
  Pallas kernels  31.9 us (96%)
  between operations  1.29 us (4%)
    pallas_call x1, Pallas kernels, on_device(): pl.pallas_call(kernel, name='restart_check', out_shape=(pltpu.VMEM((OWN,...  31.2 us

profile of v5, /device:TPU:1, one launch (start us, length us, event | category | flops | bytes accessed | tf_op | source)
XLA Modules:
  0.0 33.2 jit_solution(14221754070582270270)
XLA Ops:
  1.3 31.2 %restart_check.1 = (f32[64,128]{1,0:T(8,128)S(1)}, f32[64,128]{1,0:T(8,128)S(1)}, f32[2,3]{1,0:T(2,128)S(1)}) custom-call(s32[1,16]{1,0:T(1,128)} %bitcast.38, s32[1,16]{1,0:T(1,128)} %bitcast.39, s32[1,1]{1,0:T(1,128)S(6)} %copy.19.count_hbm, f32[16,512,512]{2,1,0:T(8,128)} %bitcast.29, f32[64,128]{1,0:T(8,128)} %bitcast.36, f32[64,128]{1,0:T(8,128)} %bitcast.37, ...), custom_call_target="tpu_custom_call" | custom-call | tf_op jit(solution)/shard_map/restart_check/pallas_call | solution.py:461
  32.5 0.7 %flush.1 = (f32[64,128]{1,0:T(8,128)}, f32[64,128]{1,0:T(8,128)}, f32[2,3]{1,0:T(2,128)}) custom-call(f32[64,128]{1,0:T(8,128)S(1)} %get-tuple-element.9.a, f32[64,128]{1,0:T(8,128)S(1)} %get-tuple-element.10.b, f32[2,3]{1,0:T(2,128)S(1)} %get-tuple-element.11.c), custom_call_target="tpu_custom_call" | custom-call | tf_op jit(solution)/shard_map/flush/pallas_call | solution.py:516

commit v6 on v5

--- a/solution.py
+++ b/solution.py
@@ -187,14 +187,14 @@
     ridx = jnp.full((8, 128), -1, jnp.int32)
     cidx = jnp.full((8, 128), -1, jnp.int32)
     for t in range(SLOTS):
-        here = (lax.rem(lane, SLOTS) == t) & (lane < 3 * SLOTS) & (jnp.full((8, 128), t, jnp.int32) < count)
+        here = (lax.rem(lane, SLOTS) == t) & (lane < 2 * SLOTS) & (jnp.full((8, 128), t, jnp.int32) < count)
         ridx = jnp.where(here, tab[0, 0, t], ridx)
         cidx = jnp.where(here, tab[1, 0, t], cidx)
     p_iota = lax.broadcasted_iota(jnp.int32, (ROW_BLOCKS, 128), 0)
     r_iota = ((p_iota // 8 % 8) * 2 + p_iota // 64) * 8 + p_iota % 8
     c_iota = lax.broadcasted_iota(jnp.int32, (COL_BLOCKS, 128), 0)
-    r_hot = jnp.where(r_iota == ridx[:1], 1.0, 0.0).astype(BF16)[:, : 3 * SLOTS]
-    c_hot = jnp.where(c_iota == cidx[:1], 1.0, 0.0).astype(BF16)[:, : 3 * SLOTS]
+    r_hot = jnp.where(r_iota == ridx[:1], 1.0, 0.0).astype(BF16)[:, : 2 * SLOTS]
+    c_hot = jnp.where(c_iota == cidx[:1], 1.0, 0.0).astype(BF16)[:, : 2 * SLOTS]
 
     pl.semaphore_wait(barrier, len(near))
 
@@ -247,30 +247,27 @@
         for d in (1, 3):
             place(yg, at, "y_d", (z, yh, yl, up4(x, d), c))
     place(yg, at, "y_d", other)
-    convert(6, 7, 8)
+    convert(6, 7)
     arrived(yg.at[pl.ds(0, 8)], "y_x2")
     at = (yl * 4 + up4(x, 2)) * 2 + core
     for c in (core, 1 - core):
         place(yg, at, "y_d", (z, yh, 1 - yl, x, c))
     place(yg, at, "y_d", other)
-    convert(9)
+    convert(8, 9)
     arrived(xg.at[pl.ds(0, 8)], "x_far")
     for d in (2, 1, 3):
         place(xg, z * 2 + 1 - yh, "x_z", z_dev(d))
+    convert(10, 11)
     arrived(yg.at[pl.ds(0, 16)], "y_x")
     for d in (1, 3):
         place(yg, (yl * 4 + up4(x, d)) * 2 + core, "y_d", other)
-    convert(*range(10, SLOTS))
+    convert(*range(12, SLOTS))
 
     def scatter(hot, dest, blocks, base, rows):
         cols = []
         for e in rows:
             v = pbuf[pl.ds(e, SLOTS, stride=8), :]
-            hi = v.astype(BF16)
-            rest = v - hi.astype(F32)
-            mid = rest.astype(BF16)
-            lo = (rest - mid.astype(F32)).astype(BF16)
-            cols.append(jnp.concatenate([hi, mid, lo], axis=0))
+            cols.append(jnp.concatenate(split2(v), axis=0))
         rhs = jnp.concatenate(cols, axis=1)
         out = jnp.dot(hot, rhs, preferred_element_type=F32)
         for i in range(len(rows)):

time: 33.4 us -> 33.4 us (level)
  no operation moved by 1% of the time
where the time goes in v6:
time: 33.4 us; the launch traced here: 33.2 us
  Pallas kernels  31.9 us (96%)
  between operations  1.29 us (4%)
    pallas_call x1, Pallas kernels, on_device(): pl.pallas_call(kernel, name='restart_check', out_shape=(pltpu.VMEM((OWN,...  31.3 us

profile of v6, /device:TPU:1, one launch (start us, length us, event | category | flops | bytes accessed | tf_op | source)
XLA Modules:
  0.0 33.2 jit_solution(15285120388396822683)
XLA Ops:
  1.3 31.3 %restart_check.1 = (f32[64,128]{1,0:T(8,128)S(1)}, f32[64,128]{1,0:T(8,128)S(1)}, f32[2,3]{1,0:T(2,128)S(1)}) custom-call(s32[1,16]{1,0:T(1,128)} %bitcast.38, s32[1,16]{1,0:T(1,128)} %bitcast.39, s32[1,1]{1,0:T(1,128)S(6)} %copy.19.count_hbm, f32[16,512,512]{2,1,0:T(8,128)} %bitcast.29, f32[64,128]{1,0:T(8,128)} %bitcast.36, f32[64,128]{1,0:T(8,128)} %bitcast.37, ...), custom_call_target="tpu_custom_call" | custom-call | tf_op jit(solution)/shard_map/restart_check/pallas_call | solution.py:458
  32.5 0.7 %flush.1 = (f32[64,128]{1,0:T(8,128)}, f32[64,128]{1,0:T(8,128)}, f32[2,3]{1,0:T(2,128)}) custom-call(f32[64,128]{1,0:T(8,128)S(1)} %get-tuple-element.9.a, f32[64,128]{1,0:T(8,128)S(1)} %get-tuple-element.10.b, f32[2,3]{1,0:T(2,128)S(1)} %get-tuple-element.11.c), custom_call_target="tpu_custom_call" | custom-call | tf_op jit(solution)/shard_map/flush/pallas_call | solution.py:513
